TPU v7x, 256 devices: a whole 4x4x8 slice. The times are simulated.
256 devices in a mesh: dp: 64 (over x, z_lo, y, core), sub: 4 (over z_hi).
Axes of the slice: x: 4, y: 4, z: 8 (z_hi: 4, z_lo: 2; z = z_hi * 2 + z_lo), core: 2. Of those that a mesh axis runs over, the one named last changes fastest.
Arguments:
- queries: float32 [16384, 1024], P(('dp', 'sub')), may hold values from -8 to 8
- passages: float32 [16384, 1024], P(('dp', 'sub')), may hold values from -8 to 8
- positives: int32 [16384], P(('dp', 'sub')), may hold values from 0 to 16383, each once
Outputs:
- losses: float32 [16384], P(('dp', 'sub'))
- query_grads: float32 [16384, 1024], P(('dp', 'sub'))
- passage_grads: float32 [16384, 1024], P(('dp', 'sub'))
All inputs are finite; a program needn't handle non-finite values.
Results may differ from a plain program's by a relative error of at most 0.00185.
The roundings to bfloat16 on the way count: a program that leaves them out, or rounds other values in their place, can miss the bound.
Values may be sent and summed in bfloat16 or wider, within the bound.
A program may use at most 128 MiB of HBM per device.

v0:
```python
import jax
import jax.numpy as jnp
from jax import lax
from jax.sharding import Mesh
from jax.sharding import PartitionSpec as P

DP = ("dp_0", "dp_1", "dp_2", "dp_3")
DP_SUB = ("dp_0", "dp_1", "dp_2", "dp_3", "sub")


logit_scale = 20.0


def laid_out(blocks, dim):
    blocks = jnp.moveaxis(blocks, 0, dim)
    lengths = blocks.shape
    return blocks.reshape(*lengths[:dim], lengths[dim] * lengths[dim + 1], *lengths[dim + 2 :])


def sent_to_all(value, axis):
    devices = lax.axis_size(axis)
    return lax.all_to_all(
        jnp.broadcast_to(value[None], (devices, *value.shape)), axis, 0, 0, tiled=True
    )


def collect(value, axis, dim):
    return laid_out(sent_to_all(value, axis), dim)


def gathered_once(value, axis):
    leaves = jax.tree.leaves(value)
    sequence = sorted(range(len(leaves)), key=lambda k: -leaves[k].size)
    width = (1, *leaves[sequence[0]].shape)[-1]
    lines = [
        jnp.pad(leaves[k].reshape(-1), (0, -leaves[k].size % width)).reshape(-1, width)
        for k in sequence
    ]
    both, at, found = (sent_to_all(jnp.concatenate(lines), axis), 0, {})
    for k, line in zip(sequence, lines):
        slab = both[:, at : at + len(line)].reshape(len(both), -1)
        found[k] = slab[:, : leaves[k].size].reshape(-1, *leaves[k].shape)
        at += len(line)
    numbers = iter(range(len(leaves)))
    return jax.tree.map(lambda _: found[next(numbers)], value)


def folded_in_pairs(pieces, combine):
    while len(jax.tree.leaves(pieces)[0]) > 1:
        pieces = jax.vmap(combine)(
            *(jax.tree.map(lambda part: part[side::2], pieces) for side in (0, 1))
        )
    return jax.tree.map(lambda part: part[0], pieces)


def joined_all(value, axis, combine):
    pieces = gathered_once(value, axis)
    return folded_in_pairs(pieces, combine)


def split_up(value, dim, devices):
    before, after = (value.shape[:dim], value.shape[dim + 1 :])
    return jnp.moveaxis(value.reshape(*before, devices, -1, *after), dim, 0)


def sum_at_owner(value, axis, dim):
    devices = lax.axis_size(axis)
    blocks = lax.all_to_all(split_up(value, dim, devices), axis, 0, 0, tiled=True)
    return jnp.sum(blocks, axis=0)


def scatter_pairs(value, chips, core, dim):
    sizes = (lax.axis_size(chips), lax.axis_size(core))
    blocks = split_up(value, dim, sizes[0] * sizes[1])
    inside = blocks.shape[1:]
    blocks = blocks.reshape(*sizes, *inside).swapaxes(0, 1).reshape(-1, *inside)
    blocks = lax.psum_scatter(blocks, core, scatter_dimension=0, tiled=True)
    return lax.psum_scatter(blocks, chips, scatter_dimension=0, tiled=True)[0]


def combine_rows(earlier, later):
    highest = jnp.maximum(earlier[0], later[0])
    exp_total = earlier[1] * jnp.exp(earlier[0] - highest) + later[1] * jnp.exp(later[0] - highest)
    return (highest, exp_total, earlier[2] + later[2])


def row_scores(query_rows, passage_rows):
    return (
        lax.dot_general(
            query_rows, passage_rows, (((1,), (1,)), ((), ())), preferred_element_type=jnp.float32
        )
        * logit_scale
    )


def local_stats(scores, onehot):
    highest = jnp.max(scores, axis=1)
    exp_total = jnp.sum(jnp.exp(scores - highest[:, None]), axis=1)
    positive_score = jnp.sum(onehot * scores, axis=1)
    return (highest, exp_total, positive_score)


def body(queries, passages, positives):
    row_count = queries.shape[0]
    groups = lax.axis_size("sub")
    member = lax.axis_index("sub")
    query_half = queries.astype(jnp.bfloat16)
    passage_half = passages.astype(jnp.bfloat16)
    query_rows, row_targets = (collect(query_half, "sub", 0), collect(positives, "sub", 0))
    width_cols = row_count * lax.axis_size(DP)
    passage_rows = lax.all_gather(passage_half, DP, axis=0, tiled=True)
    scores = row_scores(query_rows, passage_rows)
    column = jnp.arange(width_cols, dtype=jnp.int32)
    column_ids = (column // row_count * groups + member) * row_count + column % row_count
    onehot = (column_ids[None, :] == row_targets[:, None]).astype(jnp.float32)
    highest, exp_total, positive_score = local_stats(scores, onehot)
    highest, exp_total, positive_score = joined_all(
        (highest, exp_total, positive_score), "sub", combine_rows
    )
    log_norm = highest + jnp.log(exp_total)
    losses = lax.dynamic_slice_in_dim(log_norm - positive_score, member * row_count, row_count)
    weights = ((jnp.exp(scores - log_norm[:, None]) - onehot) * logit_scale).astype(jnp.bfloat16)
    query_terms = jnp.dot(weights, passage_rows, preferred_element_type=jnp.float32)
    query_grads = sum_at_owner(query_terms, "sub", 0)
    passage_grads = scatter_pairs(
        lax.dot_general(
            weights, query_rows, (((0,), (0,)), ((), ())), preferred_element_type=jnp.float32
        ),
        ("dp_0", "dp_1", "dp_2"),
        "dp_3",
        0,
    )
    return (losses, query_grads, passage_grads)


def solution(mesh):
    torus = Mesh(
        mesh.devices.reshape(4, 2, 4, 2, mesh.shape["sub"]), ("dp_0", "dp_1", "dp_2", "dp_3", "sub")
    )
    placed = (P(DP_SUB, None), P(DP_SUB, None), P(DP_SUB))
    return jax.shard_map(
        body,
        mesh=torus,
        in_specs=placed,
        out_specs=(P(DP_SUB), P(DP_SUB, None), P(DP_SUB, None)),
        check_vma=False,
    )
```

profile of v0, /device:TPU:64, one launch (start us, length us, event | category | flops | bytes accessed | tf_op | source)
XLA Modules:
  0.0 401.1 jit_solution(4751008625709761402)
XLA Ops:
  7.2 0.0 all-gather.2.cloned.1.call-start
  7.2 1.6 convert_element_type.19
  8.8 0.0 all-gather.2.cloned.1.call-update
  8.9 1.2 broadcast_in_dim.7
  10.1 8.1 %all-to-all-start.1 = ((s32[4,1,64]{2,1,0:T(1,128)}), s32[4,1,64]{2,1,0:T(1,128)S(1)}, u32[]{:S(2)}, u32[]{:S(2)}) async-start(s32[4,1,64]{2,1,0:T(1,128)} %broadcast_in_dim.7), calls=%async_computation.1 | async-start | bytes 4096 | tf_op jit(solution)/shard_map/all_to_all | solution.py:22
  18.2 1.0 convert_element_type.18
  19.2 4.3 %all-to-all-done.1 = s32[4,1,64]{2,1,0:T(1,128)S(1)} async-done(((s32[4,1,64]{2,1,0:T(1,128)}), s32[4,1,64]{2,1,0:T(1,128)S(1)}, u32[]{:S(2)}, u32[]{:S(2)}) %all-to-all-start.1) | async-done | bytes 1056 | tf_op jit(solution)/shard_map/all_to_all | solution.py:22
  23.5 0.8 broadcast_in_dim.6
  24.3 5.8 %all-to-all-start = ((bf16[4,64,1024]{2,1,0:T(8,128)(2,1)}), bf16[4,64,1024]{2,1,0:T(8,128)(2,1)S(1)}, u32[]{:S(2)}, u32[]{:S(2)}) async-start(bf16[4,64,1024]{2,1,0:T(8,128)(2,1)} %broadcast_in_dim.6), calls=%async_computation | async-start | bytes 1048576 | tf_op jit(solution)/shard_map/all_to_all | solution.py:22
  30.1 0.5 broadcast.96
  30.6 0.7 reduce.3
  31.3 0.1 eq.25
  31.4 17.7 %all-to-all-done = bf16[4,64,1024]{2,1,0:T(8,128)(2,1)S(1)} async-done(((bf16[4,64,1024]{2,1,0:T(8,128)(2,1)}), bf16[4,64,1024]{2,1,0:T(8,128)(2,1)S(1)}, u32[]{:S(2)}, u32[]{:S(2)}) %all-to-all-start) | async-done | bytes 524320 | tf_op jit(solution)/shard_map/all_to_all | solution.py:22
  49.1 79.8 %all-gather.2.cloned.1.call-done = bf16[4096,1024]{1,0:T(8,128)(2,1)} async-done(((bf16[64,1024]{1,0:T(8,128)(2,1)}), bf16[4096,1024]{1,0:T(8,128)(2,1)}) %all-gather.2.cloned.1.call-update) | async-done | bytes 8388624 | tf_op jit(solution)/shard_map/all_gather | solution.py:111
  128.9 5.9 %fusion.27 = (f32[256]{0:T(256)S(1)}, f32[256,4096]{1,0:T(8,128)S(1)}) fusion(bf16[256,1024]{1,0:T(8,128)(2,1)S(1)} %bitcast.36, bf16[4096,1024]{1,0:T(8,128)(2,1)} %all-gather.2.cloned.1.call-done), kind=kOutput, calls=%fused_computation.47 | convolution fusion | flops 2149580544 | bytes 13108224 | tf_op jit(solution)/shard_map/dot_general | solution.py:89
  134.8 2.0 copy-done
  136.9 1.1 exponential_reduce_fusion
  138.0 11.9 %all_to_all.21 = f32[4,3,256]{2,1,0:T(4,128)S(1)} all-to-all(f32[4,3,256]{2,1,0:T(4,128)S(1)} %broadcast_in_dim.8), channel_id=1, replica_groups=mesh['dp_0'=4,'dp_1'=2,'dp_2'=4,'dp_3'=2,'sub'=4] {'sub'}, dimensions={0} | all-to-all | bytes 24576 | tf_op jit(solution)/shard_map/all_to_all | solution.py:22
  150.0 4.7 %fusion.5 = bf16[4096,256]{0,1:T(8,128)(2,1)} fusion(f32[256,4096]{1,0:T(8,128)} %copy-done, s32[4096]{0:T(1024)S(1)} %fusion.21, f32[256]{0:T(256)S(1)} %bitcast.40, s32[256]{0:T(256)S(1)} %eq.25), kind=kLoop, calls=%fused_computation.10 | loop fusion | flops 6291456 | bytes 6309888 | tf_op jit(solution)/shard_map/convert_element_type | solution.py:122
  154.8 3.3 copy.9
  158.0 2.3 convolution_bitcast_fusion
  160.4 6.0 %copy.10 = f32[2,32,64,1024]{3,2,1,0:T(8,128)} copy(f32[2,32,64,1024]{3,2,0,1:T(8,128)S(1)} %convolution_bitcast_fusion) | data formatting | bytes 33554432 | tf_op jit(solution)/shard_map/transpose | solution.py:76
  166.4 0.0 reduce-scatter.3.cloned.1.call-update
  166.5 0.0 reduce-scatter.5.cloned.1.call-start
  166.5 27.7 %reduce-scatter.3.cloned.1.call-done = f32[32,64,1024]{2,1,0:T(8,128)} async-done(((f32[64,64,1024]{2,1,0:T(8,128)}), f32[32,64,1024]{2,1,0:T(8,128)}) %reduce-scatter.3.cloned.1.call-update) | async-done | bytes 8388624 | tf_op jit(solution)/shard_map/reduce_scatter | solution.py:77
  194.3 0.0 reduce-scatter.5.cloned.1.call-update
  194.3 8.1 %fusion.6 = f32[256,1024]{1,0:T(8,128)} fusion(bf16[4096,1024]{1,0:T(8,128)(2,1)} %all-gather.2.cloned.1.call-done, f32[256,4096]{1,0:T(8,128)} %copy-done, f32[256]{0:T(256)S(1)} %bitcast.41, s32[4096]{0:T(1024)S(1)} %fusion.21, s32[256]{0:T(256)S(1)} %eq.25), kind=kOutput, calls=%fused_computation.13 | convolution fusion | flops 2153775104 | bytes 13649920 | tf_op jit(solution)/shard_map/dot_general | solution.py:123
  202.4 7.4 %all-to-all-start.3 = ((f32[4,64,1024]{2,1,0:T(8,128)}), f32[4,64,1024]{2,1,0:T(8,128)S(1)}, u32[]{:S(2)}, u32[]{:S(2)}) async-start(f32[4,64,1024]{2,1,0:T(8,128)} %bitcast.7), calls=%async_computation.3 | async-start | bytes 2097152 | tf_op jit(solution)/shard_map/all_to_all | solution.py:68
  209.8 0.6 dynamic_slice.3
  210.4 35.8 %all-to-all-done.3 = f32[4,64,1024]{2,1,0:T(8,128)S(1)} async-done(((f32[4,64,1024]{2,1,0:T(8,128)}), f32[4,64,1024]{2,1,0:T(8,128)S(1)}, u32[]{:S(2)}, u32[]{:S(2)}) %all-to-all-start.3) | async-done | bytes 1048608 | tf_op jit(solution)/shard_map/all_to_all | solution.py:68
  246.2 0.8 reduce_sum.29
  247.0 147.6 %reduce-scatter.5.cloned.1.call-done = f32[1,64,1024]{2,1,0:T(8,128)} async-done(((f32[32,64,1024]{2,1,0:T(8,128)}), f32[1,64,1024]{2,1,0:T(8,128)}) %reduce-scatter.5.cloned.1.call-update) | async-done | bytes 262160 | tf_op jit(solution)/shard_map/reduce_scatter | solution.py:78
  (19 shorter events, 0.3 us)
Async XLA Ops:
  7.2 121.8 %all-gather.2.cloned.1.call-start = ((), (), s32[]{:S(2)}) async-start(), calls=%async_computation.6 | async-start | bytes 8519680 | tf_op jit(solution)/shard_map/all_gather | solution.py:111
  10.1 13.4 %all-to-all-start.1 = ((s32[4,1,64]{2,1,0:T(1,128)}), s32[4,1,64]{2,1,0:T(1,128)S(1)}, u32[]{:S(2)}, u32[]{:S(2)}) async-start(s32[4,1,64]{2,1,0:T(1,128)} %broadcast_in_dim.7), calls=%async_computation.1 | async-start | bytes 4096 | tf_op jit(solution)/shard_map/all_to_all | solution.py:22
  24.3 24.8 %all-to-all-start = ((bf16[4,64,1024]{2,1,0:T(8,128)(2,1)}), bf16[4,64,1024]{2,1,0:T(8,128)(2,1)S(1)}, u32[]{:S(2)}, u32[]{:S(2)}) async-start(bf16[4,64,1024]{2,1,0:T(8,128)(2,1)} %broadcast_in_dim.6), calls=%async_computation | async-start | bytes 1048576 | tf_op jit(solution)/shard_map/all_to_all | solution.py:22
  30.1 164.1 %reduce-scatter.3.cloned.1.call-start = ((), (), s32[]{:S(2)}) async-start(), calls=%async_computation.7 | async-start | bytes 25165824 | tf_op jit(solution)/shard_map/reduce_scatter | solution.py:77
  134.8 2.0 copy-start
  166.5 228.1 %reduce-scatter.5.cloned.1.call-start = ((), (), s32[]{:S(2)}) async-start(), calls=%async_computation.8 | async-start | bytes 8650752 | tf_op jit(solution)/shard_map/reduce_scatter | solution.py:78
  202.4 43.8 %all-to-all-start.3 = ((f32[4,64,1024]{2,1,0:T(8,128)}), f32[4,64,1024]{2,1,0:T(8,128)S(1)}, u32[]{:S(2)}, u32[]{:S(2)}) async-start(f32[4,64,1024]{2,1,0:T(8,128)} %bitcast.7), calls=%async_computation.3 | async-start | bytes 2097152 | tf_op jit(solution)/shard_map/all_to_all | solution.py:68
Sparse Core Ops, SparseCore 0:
  10.4 118.4 all-gather.1
  166.6 27.6 reduce-scatter.2
  197.4 197.0 reduce-scatter.4
where the time goes:
time: 402 us; the launch traced here: 401 us
  waiting for transfers between devices  313 us (78%)
  starting transfers between devices  21.4 us (5%)
  matrix products  16.3 us (4%)
  local copies, waits for them, and re-layouts  14.8 us (4%)
  between operations  13.8 us (3%)
  blocking collectives  11.9 us (3%)
  other arithmetic  9.91 us (2%)
    reduce_scatter x1, waiting for transfers between devices, scatter_pairs(): return lax.psum_scatter(blocks, chips, scatter_dimension=0, tiled=True)[0]  148 us
    all_gather x1, waiting for transfers between devices, body(): passage_rows = lax.all_gather(passage_half, DP, axis=0, tiled=True)  79.8 us
    all_to_all x1, waiting for transfers between devices, sum_at_owner(): lax.all_to_all(split_up(value, dim, devices), axis, 0, 0, tiled=True)  35.8 us
    reduce_scatter x1, waiting for transfers between devices, scatter_pairs(): blocks = lax.psum_scatter(blocks, core, scatter_dimension=0, tiled=True)  27.7 us
    all_to_all x2, waiting for transfers between devices, sent_to_all(): lax.all_to_all(jnp.broadcast_to(value[None], (devices, *value.shape)), ax...  22 us
    all_to_all x2, starting transfers between devices, sent_to_all(): lax.all_to_all(jnp.broadcast_to(value[None], (devices, *value.shape)), ax...  13.9 us
    all_to_all x1, blocking collectives, sent_to_all(): lax.all_to_all(jnp.broadcast_to(value[None], (devices, *value.shape)), ax...  11.9 us
    dot_general x1, matrix products, body(): jnp.dot(weights, passage_rows, preferred_element_type=jnp.float32)  8.11 us
  transfers between devices with their start and end apart: 6, of which 6 were waited for; matrix products, arithmetic and copies ran while one was open for 3% of the time, Pallas kernels for 0%

commit v1 on v0

v1 whole, which is shorter than its diff:
```python
import functools

import jax
import jax.numpy as jnp
from jax import lax
from jax.experimental import pallas as pl
from jax.experimental.pallas import tpu as pltpu
from jax.sharding import Mesh
from jax.sharding import PartitionSpec as P

AXES = ("x", "zl", "y", "c", "zh")
RING = 4
logit_scale = 20.0
MESSAGES = 160


class Links:
    def __init__(self, send_sem, recv_sem, zl_size, z_size):
        self.send_sem, self.recv_sem = send_sem, recv_sem
        self.count = 0
        self.open = []
        self.x, self.y, self.c = (lax.axis_index(a) for a in ("x", "y", "c"))
        self.zl_size, self.z_size = zl_size, z_size
        self.z = lax.axis_index("zh") * zl_size + lax.axis_index("zl")

    def at(self, axis, offset):
        size = {"x": RING, "y": RING, "z": self.z_size, "c": 2}[axis]
        return lax.rem(getattr(self, axis) + (offset % size), size)

    def device(self, axis, offset):
        place = self.at(axis, offset)
        if axis == "z":
            return {"zl": lax.rem(place, self.zl_size), "zh": lax.div(place, self.zl_size)}
        return {axis: place}

    def send(self, src, dst, axis, offset):
        k = self.count
        self.count += 1
        copy = pltpu.make_async_remote_copy(
            src_ref=src,
            dst_ref=dst,
            send_sem=self.send_sem.at[k],
            recv_sem=self.recv_sem.at[k],
            device_id=self.device(axis, offset),
            device_id_type=pl.DeviceIdType.MESH,
        )
        copy.start()
        self.open.append(copy)
        return copy

    def finish(self):
        for copy in self.open:
            copy.wait_send()


def gather_plane(net, qb, first, second, rows):
    def block(a, b, part=rows):
        place = {first: net.at(first, a), second: net.at(second, b)}
        return qb.at[place["x"], place["y"], part]

    def push(ref, axis, offset):
        return net.send(ref, ref, axis, offset)

    start, length = rows.start, rows.size
    top = pl.ds(start, length // 2)
    low = pl.ds(start + length // 2, length // 2)
    own = block(0, 0)
    near = [push(own, first, s) for s in (1, -1)]
    yield
    wide = {0: [push(own, second, s) for s in (1, -1)]}
    yield
    far = []
    near[0].wait_recv()
    far.append(push(block(-1, 0, top), first, 1))
    wide[-1] = [push(block(-1, 0), second, s) for s in (1, -1)]
    near[1].wait_recv()
    far.append(push(block(1, 0, low), first, -1))
    wide[1] = [push(block(1, 0), second, s) for s in (1, -1)]
    yield
    for copy in wide[0]:
        copy.wait_recv()
    last = [push(block(0, -1), second, 1)]
    yield
    for copy in far:
        copy.wait_recv()
    wide[2] = [push(block(2, 0), second, s) for s in (1, -1)]
    yield
    for copy in wide[-1]:
        copy.wait_recv()
    last.append(push(block(-1, -1), second, 1))
    for copy in wide[1]:
        copy.wait_recv()
    last.append(push(block(1, 1), second, -1))
    yield
    for copy in wide[2]:
        copy.wait_recv()
    last.append(push(block(2, 1), second, -1))
    yield
    for copy in last:
        copy.wait_recv()
    yield


def gather_line(net, pb, rows):
    half = rows // 2
    parts = (pl.ds(0, half), pl.ds(half, half))
    reach = net.z_size // 2
    across = []

    def hand_over(offset, part):
        across.append(
            net.send(
                pb.at[0, net.at("z", offset), part], pb.at[1, net.at("z", offset), part], "c", 1
            )
        )

    def push(offset, part, direction):
        ref = pb.at[0, net.at("z", offset), part]
        return net.send(ref, ref, "z", direction)

    flights = {(d, h): push(0, parts[h], d) for h in (0, 1) for d in (1, -1)}
    for part in parts:
        hand_over(0, part)
    yield
    for step in range(1, reach + 1):
        ahead = {}
        for h in (0, 1):
            for d in (1, -1):
                carried = 0 if d == 1 else 1
                if step == reach and h != carried:
                    continue
                flights[d, h].wait_recv()
                if step < reach - 1 or (step == reach - 1 and h == carried):
                    ahead[d, h] = push(-d * step, parts[h], d)
                hand_over(-d * step, parts[h])
        flights = ahead
        yield
    for copy in across:
        copy.wait_recv()
    yield


def exchange(net, axis, src, slots):
    copies = [net.send(src, slots.at[k - 1], axis, k) for k in (1, 2, 3)]
    for copy in copies:
        copy.wait_recv()


def scatter_plane(net, total, landing, late, first, second):
    def block(a, b, part=slice(None)):
        place = {first: net.at(first, a), second: net.at(second, b)}
        return total.at[place["x"], place["y"], part]

    front, back = (1, 0), (2, 3)
    far = {}
    for a, b in zip(front, back):
        far[1, a] = net.send(block(2, a), landing.at[0, a], first, 1)
        far[-1, b] = net.send(block(2, b), landing.at[1, b], first, -1)
    yield
    near = {}
    for a, b in zip(front, back):
        near[1, b] = net.send(block(1, b), landing.at[2, b], first, 1)
        near[-1, a] = net.send(block(-1, a), landing.at[3, a], first, -1)
    yield
    for a, b in zip(front, back):
        for d, k, lane in ((1, a, 0), (-1, b, 1)):
            far[d, k].wait_recv()
            ref = block(d, k)
            ref[...] += landing[lane, k]
            near[d, k] = net.send(ref, landing.at[2 + lane, k], first, d)
    yield
    half = total.shape[2] // 2
    top, low = pl.ds(0, half), pl.ds(half, half)
    hops = {}
    for k in (2, 1, 3, 0):
        near[1, k].wait_recv()
        near[-1, k].wait_recv()
        ref = block(0, k)
        ref[...] += landing[2, k] + landing[3, k]
        if k == 2:
            hops[1, 0] = net.send(block(0, 2, top), late.at[0, top], second, 1)
            hops[-1, 0] = net.send(block(0, 2, low), late.at[0, low], second, -1)
        if k == 1:
            hops[1, 1] = net.send(block(0, 1, low), late.at[1, low], second, 1)
        if k == 3:
            hops[-1, 1] = net.send(block(0, -1, top), late.at[2, top], second, -1)
    yield
    for d, part, slot in ((1, top, 1), (-1, low, 2)):
        hops[d, 0].wait_recv()
        ref = block(0, d, part)
        ref[...] += late[0, part]
        hops[d, 2] = net.send(ref, late.at[slot, part], second, d)
    yield
    for d in (1, -1):
        hops[d, 1].wait_recv()
        hops[d, 2].wait_recv()
    ref = block(0, 0)
    ref[...] += late[1] + late[2]
    yield


def scatter_line(net, total, across, landing, rows):
    reach = net.z_size // 2
    half = rows // 2
    parts = (pl.ds(0, half), pl.ds(half, half))
    order = [reach]
    for k in range(reach - 1, 0, -1):
        order += [k, -k]
    order.append(0)
    gifts = {}
    for k in order:
        place = net.at("z", k)
        gifts[k] = net.send(total.at[1, place], across.at[place], "c", 1)
    yield

    def settle(k):
        gifts[k].wait_recv()
        place = net.at("z", k)
        total[0, place] += across[place]

    flights = {}

    def push(d, h, step):
        flights[d, h] = net.send(
            total.at[0, net.at("z", d * (reach - step)), parts[h]],
            landing.at[0 if d == 1 else 1, step, parts[h]],
            "z",
            d,
        )

    settle(reach)
    push(1, 0, 0)
    push(-1, 1, 0)
    settle(reach - 1)
    push(1, 1, 1)
    settle(1 - reach)
    push(-1, 0, 1)
    yield
    for step in range(1, reach):
        if step > 1:
            settle(reach - step)
            settle(step - reach)
        for h in (0, 1):
            for d in (1, -1):
                full = (d == 1) == (h == 0)
                if not full and step == 1:
                    continue
                flights[d, h].wait_recv()
                total[0, net.at("z", d * (reach - step)), parts[h]] += landing[
                    0 if d == 1 else 1, step - 1, parts[h]
                ]
                push(d, h, step)
        yield
    settle(0)
    for copy in flights.values():
        copy.wait_recv()
    yield


def interleave(*rounds):
    rounds = list(rounds)
    while rounds:
        for r in list(rounds):
            try:
                next(r)
            except StopIteration:
                rounds.remove(r)


def kernel(
    zl_size,
    z_size,
    q_in,
    p_in,
    t_in,
    loss_out,
    qg_out,
    pg_out,
    qb,
    pb,
    tb,
    scores,
    weights,
    stats,
    stats_x,
    mid,
    stats_y,
    qga,
    qgb,
    pg,
    land_a,
    land_b,
    late_a,
    late_b,
    across,
    land_z,
    send_sem,
    recv_sem,
):
    rows, width = q_in.shape
    net = Links(send_sem, recv_sem, zl_size, z_size)
    peers = [("x", k) for k in (1, 2, 3)] + [("y", k) for k in (1, 2, 3)]
    peers += [("z", k) for k in sorted({1, z_size - 1})] + [("c", 1)]
    barrier = pltpu.get_barrier_semaphore()
    for axis, k in peers:
        pl.semaphore_signal(
            barrier,
            inc=1,
            device_id=net.device(axis, k),
            device_id_type=pl.DeviceIdType.MESH,
        )
    qb[net.x, net.y] = q_in[...].astype(jnp.bfloat16)
    pb[0, net.z] = p_in[...].astype(jnp.bfloat16)
    mine = t_in[...]
    tb[net.x, net.y] = jnp.broadcast_to(jnp.concatenate([mine] * (128 // rows), axis=1), (8, 128))
    pl.semaphore_wait(barrier, len(peers))

    half = rows // 2
    interleave(
        gather_plane(net, qb, "x", "y", pl.ds(0, half)),
        gather_plane(net, qb, "y", "x", pl.ds(half, half)),
        gather_line(net, pb, rows),
    )
    tile = tb.at[net.x, net.y]
    copies = [net.send(tile, tile, "x", k) for k in (1, 2, 3)]
    for copy in copies:
        copy.wait_recv()
    column = tb.at[:, net.y]
    copies = [net.send(column, column, "y", k) for k in (1, 2, 3)]
    for copy in copies:
        copy.wait_recv()

    group = RING * rows
    columns = 2 * z_size * rows
    band = 128
    bands = columns // band

    def target_of(xs):
        value = jnp.concatenate([tb[xs, ys, 0:1, 0:rows] for ys in range(RING)], axis=1)
        inside = lax.rem(value, rows)
        value = lax.div(value, rows)
        zh_size = z_size // zl_size
        zh = lax.rem(value, zh_size)
        value = lax.div(value, zh_size)
        core = lax.rem(value, 2)
        value = lax.div(value, 2)
        y = lax.rem(value, RING)
        value = lax.div(value, RING)
        zl = lax.rem(value, zl_size)
        x = lax.div(value, zl_size)
        local = (lax.rem(core + net.c, 2) * z_size + zh * zl_size + zl) * rows + inside
        return jnp.where((x == net.x) & (y == net.y), local, -1)

    all_passages = pb[...].reshape(columns, width)
    for xs in range(RING):
        queries = qb[xs].reshape(group, width)
        scores[xs] = (
            lax.dot_general(
                all_passages, queries, (((1,), (1,)), ((), ())), preferred_element_type=jnp.float32
            )
            * logit_scale
        )
    fold = lambda value, how: how(value.reshape(band // 8, 8, group), axis=0)
    for xs in range(RING):
        target = target_of(xs)

        def top(b, highest):
            return jnp.maximum(highest, fold(scores[xs, pl.ds(b * band, band)], jnp.max))

        highest = lax.fori_loop(0, bands, top, jnp.full((8, group), -jnp.inf, jnp.float32))
        highest = jnp.max(highest, axis=0, keepdims=True)

        def terms(b, totals):
            piece = pl.ds(b * band, band)
            value = scores[xs, piece]
            place = lax.broadcasted_iota(jnp.int32, (band, group), 0) + b * band
            hit = jnp.where(place == target, value, 0.0)
            value = jnp.exp(value - highest)
            scores[xs, piece] = value
            return totals[0] + fold(value, jnp.sum), totals[1] + fold(hit, jnp.sum)

        zero = jnp.zeros((8, group), jnp.float32)
        total, hit = lax.fori_loop(0, bands, terms, (zero, zero))
        stats[xs : xs + 1] = highest
        stats[RING + xs : RING + xs + 1] = jnp.sum(total, axis=0, keepdims=True)
        stats[2 * RING + xs : 2 * RING + xs + 1] = jnp.sum(hit, axis=0, keepdims=True)
    stats[3 * RING :] = jnp.zeros((RING, group), jnp.float32)

    def combined(own, others):
        pieces = [own[...]] + [others[k] for k in range(3)]
        tops = [piece[:RING] for piece in pieces]
        highest = functools.reduce(jnp.maximum, tops)
        total = sum(
            piece[RING : 2 * RING] * jnp.exp(top - highest) for piece, top in zip(pieces, tops)
        )
        positive = sum(piece[2 * RING : 3 * RING] for piece in pieces)
        return highest, total, positive

    exchange(net, "x", stats, stats_x)
    highest, total, positive = combined(stats, stats_x)
    mid[0:RING] = highest
    mid[RING : 2 * RING] = total
    mid[2 * RING : 3 * RING] = positive
    mid[3 * RING :] = jnp.zeros((RING, group), jnp.float32)
    exchange(net, "y", mid, stats_y)
    highest, total, positive = combined(mid, stats_y)
    log_norm = highest + jnp.log(total)
    losses = log_norm - positive
    line = lax.broadcasted_iota(jnp.int32, losses.shape, 0)
    losses = jnp.sum(jnp.where(line == net.x, losses, 0.0), axis=0, keepdims=True)
    picked = losses[:, :rows]
    for ys in range(1, RING):
        picked = jnp.where(net.y == ys, losses[:, ys * rows : (ys + 1) * rows], picked)
    loss_out[...] = picked
    factor = jnp.exp(stats[0:RING] - log_norm)

    for xs in range(RING):
        target = target_of(xs)
        scale = factor[xs : xs + 1]

        def weigh(b, carry):
            piece = pl.ds(pl.multiple_of(b * band, band), band)
            place = lax.broadcasted_iota(jnp.int32, (band, group), 0) + b * band
            onehot = jnp.where(place == target, 1.0, 0.0)
            weights[piece, xs * group : (xs + 1) * group] = (
                (scores[xs, piece] * scale - onehot) * logit_scale
            ).astype(jnp.bfloat16)
            return carry

        lax.fori_loop(0, bands, weigh, 0)

    all_queries = qb[...].reshape(RING * group, width)
    for core in (1, 0):
        some = weights[core * z_size * rows : (core + 1) * z_size * rows]
        pg[core] = jnp.dot(some, all_queries, preferred_element_type=jnp.float32).reshape(
            z_size, rows, width
        )
    for xs in range(RING):
        some = weights[:, xs * group : (xs + 1) * group]
        part = lax.dot_general(
            some, all_passages, (((0,), (0,)), ((), ())), preferred_element_type=jnp.float32
        )
        qga[xs] = part[:, : width // 2].reshape(RING, rows, width // 2)
        qgb[xs] = part[:, width // 2 :].reshape(RING, rows, width // 2)

    interleave(
        scatter_line(net, pg, across, land_z, rows),
        scatter_plane(net, qga, land_a, late_a, "x", "y"),
        scatter_plane(net, qgb, land_b, late_b, "y", "x"),
    )
    qg_out[:, : width // 2] = qga[net.x, net.y]
    qg_out[:, width // 2 :] = qgb[net.x, net.y]
    reach = z_size // 2
    pg_out[...] = pg[0, net.z] + (land_z[0, reach - 1] + land_z[1, reach - 1])
    net.finish()


def body(zl_size, z_size, queries, passages, positives):
    rows, width = queries.shape
    group = RING * rows
    columns = 2 * z_size * rows
    f32, bf16 = jnp.float32, jnp.bfloat16
    reach = z_size // 2
    losses, query_grads, passage_grads = pl.pallas_call(
        functools.partial(kernel, zl_size, z_size),
        out_shape=(
            jax.ShapeDtypeStruct((1, rows), f32),
            jax.ShapeDtypeStruct((rows, width), f32),
            jax.ShapeDtypeStruct((rows, width), f32),
        ),
        in_specs=[pl.BlockSpec(memory_space=pltpu.VMEM)] * 3,
        out_specs=[pl.BlockSpec(memory_space=pltpu.VMEM)] * 3,
        scratch_shapes=[
            pltpu.VMEM((RING, RING, rows, width), bf16),
            pltpu.VMEM((2, z_size, rows, width), bf16),
            pltpu.VMEM((RING, RING, 8, 128), jnp.int32),
            pltpu.VMEM((RING, columns, group), f32),
            pltpu.VMEM((columns, RING * group), bf16),
            pltpu.VMEM((4 * RING, group), f32),
            pltpu.VMEM((3, 4 * RING, group), f32),
            pltpu.VMEM((4 * RING, group), f32),
            pltpu.VMEM((3, 4 * RING, group), f32),
            pltpu.VMEM((RING, RING, rows, width // 2), f32),
            pltpu.VMEM((RING, RING, rows, width // 2), f32),
            pltpu.VMEM((2, z_size, rows, width), f32),
            pltpu.VMEM((4, RING, rows, width // 2), f32),
            pltpu.VMEM((4, RING, rows, width // 2), f32),
            pltpu.VMEM((3, rows, width // 2), f32),
            pltpu.VMEM((3, rows, width // 2), f32),
            pltpu.VMEM((z_size, rows, width), f32),
            pltpu.VMEM((2, reach, rows, width), f32),
            pltpu.SemaphoreType.DMA((MESSAGES,)),
            pltpu.SemaphoreType.DMA((MESSAGES,)),
        ],
        compiler_params=pltpu.CompilerParams(
            collective_id=0, has_side_effects=True, vmem_limit_bytes=60 * 1024 * 1024
        ),
    )(queries, passages, positives.reshape(1, rows))
    return losses.reshape(rows), query_grads, passage_grads


def solution(mesh):
    zl_size, z_hi = 2, mesh.shape["sub"]
    torus = Mesh(mesh.devices.reshape(RING, zl_size, RING, 2, z_hi), AXES)
    return jax.shard_map(
        functools.partial(body, zl_size, zl_size * z_hi),
        mesh=torus,
        in_specs=(P(AXES, None), P(AXES, None), P(AXES)),
        out_specs=(P(AXES), P(AXES, None), P(AXES, None)),
        check_vma=False,
    )
```

time: 402 us -> 89.3 us (0.22)
  the two profiles are of different devices: /device:TPU:64 before, /device:TPU:1 now
where the time goes in v1:
time: 89.3 us; the launch traced here: 89.1 us
  Pallas kernels  84.9 us (95%)
  local copies, waits for them, and re-layouts  3.56 us (4%)
    pallas_call x1, Pallas kernels, body(): pl.pallas_call(functools.partial(kernel, zl_size, z_size), out_shape=(jax...  84.9 us
    unnamed x7, local copies, waits for them, and re-layouts  3.56 us

profile of v1, /device:TPU:1, one launch (start us, length us, event | category | flops | bytes accessed | tf_op | source)
XLA Modules:
  0.0 89.1 jit_solution(17663262201414676384)
XLA Ops:
  0.6 84.9 %shard_map.58 = (f32[1,64]{1,0:T(1,128)}, f32[64,1024]{1,0:T(8,128)}, f32[64,1024]{1,0:T(8,128)}) custom-call(f32[64,1024]{1,0:T(8,128)} %q_in.1, f32[64,1024]{1,0:T(8,128)} %p_in.1, s32[1,64]{1,0:T(1,128)} %bitcast.2), custom_call_target="tpu_custom_call" | custom-call | tf_op jit(solution)/shard_map/pallas_call | solution.py:464
  85.6 0.0 copy-start.1
  85.6 0.6 copy-done.1
  86.2 0.5 copy.9
  86.7 0.0 copy-start
  86.7 1.7 %copy.10 = f32[64,1024]{1,0:T(8,128)} copy(f32[64,1024]{1,0:T(8,128)} %get-tuple-element.13) | data formatting | bytes 524288
  88.4 0.0 copy-done
  88.4 0.7 copy.11
Async XLA Ops:
  85.6 0.6 copy-start.1
  86.7 1.7 %copy-start = (f32[64,1024]{1,0:T(8,128)S(1)}, f32[64,1024]{1,0:T(8,128)}, u32[]{:S(2)}) copy-start(f32[64,1024]{1,0:T(8,128)} %get-tuple-element.14) | copy-start | bytes 786436

commit v2 on v0

v2 whole, which is shorter than its diff:
```python
import functools

import jax
import jax.numpy as jnp
from jax import lax
from jax.experimental import pallas as pl
from jax.experimental.pallas import tpu as pltpu
from jax.sharding import Mesh
from jax.sharding import PartitionSpec as P

AXES = ("x", "zl", "y", "c", "zh")
RING = 4
logit_scale = 20.0
SIGNALS = 136

WIRE = {"x": 0.022, "y": 0.022, "z": 0.022, "c": 0.0016}
DELAY = {"x": 2.4, "y": 2.4, "z": 2.5, "c": 1.0}


class Place:
    def __init__(self, zl_size, z_size):
        self.x, self.y, self.c = (lax.axis_index(a) for a in ("x", "y", "c"))
        self.zl_size, self.z_size = zl_size, z_size
        self.z = lax.axis_index("zh") * zl_size + lax.axis_index("zl")

    def at(self, axis, offset):
        size = {"x": RING, "y": RING, "z": self.z_size, "c": 2}[axis]
        return lax.rem(getattr(self, axis) + (offset % size), size)

    def device(self, axis, offset):
        place = self.at(axis, offset)
        if axis == "z":
            return {"zl": lax.rem(place, self.zl_size), "zh": lax.div(place, self.zl_size)}
        return {axis: place}


class Plan:
    def __init__(self, place, recv_sem, send_sems):
        self.place, self.recv_sem, self.send_sems = place, recv_sem, send_sems
        self.tasks = []
        self.slots = {}
        self.copies = {}
        self.sent = {}

    def task(self, name, needs=(), run=None, sends=(), cost=0.05, rank=0):
        self.tasks.append((name, tuple(needs), run, tuple(sends), cost, rank))

    def order(self):
        waiting = list(enumerate(self.tasks))
        known, link, now, result = {}, {}, 0.0, []
        while waiting:
            ready = []
            for index, task in waiting:
                if all(n in known for n in task[1]):
                    ready.append((max([known[n] for n in task[1]], default=0.0), task[5], index, task))
            due = [r for r in ready if r[0] <= now]
            pick = min(due, key=lambda r: (r[1], r[2])) if due else min(ready, key=lambda r: r[:3])
            start, _, index, task = pick
            now = max(now, start) + task[4]
            known[task[0]] = now
            for message, axis, offset, kib, _, _ in task[3]:
                lane = (axis, offset)
                link[lane] = max(link.get(lane, 0.0), now) + kib * WIRE[axis]
                known[message] = link[lane] + DELAY[axis]
            waiting = [w for w in waiting if w[0] != index]
            result.append(task)
        return result

    def signal(self, message):
        kind = message.split("_")[0]
        if kind == "rs":
            kind = "qg"
        group = self.slots.setdefault(message.split("_")[0], {})
        number = group.setdefault(message, len(group))
        base = {"qg": 0, "pg": 60, "tg": 96, "st": 102, "rz": 108}[kind]
        return self.recv_sem.at[base + number]

    def run(self):
        got = set()
        for name, needs, run, sends, _, _ in self.order():
            for need in needs:
                if need in self.copies and need not in got:
                    got.add(need)
                    self.copies[need].wait_recv()
            if run is not None:
                run()
            for message, axis, offset, kib, pool, refs in sends:
                src, dst = refs()
                copy = pltpu.make_async_remote_copy(
                    src_ref=src,
                    dst_ref=dst,
                    send_sem=self.send_sems.at[pool],
                    recv_sem=self.signal(message),
                    device_id=self.place.device(axis, offset),
                    device_id_type=pl.DeviceIdType.MESH,
                )
                copy.start()
                self.copies[message] = copy
                self.sent[pool] = self.sent.get(pool, 0) + kib
        missed = set(self.copies) - got
        assert not missed, missed

    def finish(self, ref, pool, per_kib=1):
        dummy = ref.at[pl.ds(0, self.sent[pool] // per_kib)]
        pltpu.make_async_remote_copy(
            src_ref=dummy,
            dst_ref=dummy,
            send_sem=self.send_sems.at[pool],
            recv_sem=self.recv_sem.at[0],
            device_id=self.place.device("c", 1),
            device_id_type=pl.DeviceIdType.MESH,
        ).wait_send()


def slot_of(offset, z_size):
    offset = offset % z_size
    if offset == 0:
        return 0
    if offset <= z_size // 2:
        return 2 * offset - 1
    return 2 * (z_size - offset)


def plan_query_gather(plan, qb, first, second, pieces, quarter):
    place = plan.place
    kib = 32
    brings = {}

    def ref(a, b, p):
        at = {first: place.at(first, a), second: place.at(second, b)}
        return qb.at[at["x"], at["y"], pl.ds(p * quarter, quarter)]

    def send(kind, a, b, p, axis, d):
        name = f"qg_{first}{kind}{a}{p}{d}"
        to = (a - d, b) if axis == first else (a, b - d)
        key = ((to[0] + 1) % 4 - 1, (to[1] + 1) % 4 - 1)
        brings.setdefault(key, []).append(name)
        both = lambda: (ref(a, b, p),) * 2
        return name, (name, axis, d, kib, 0, both)

    u, v = pieces
    opening, names = [], {}
    for p in pieces:
        for d in (1, -1):
            names["f", p, d], s = send("f", 0, 0, p, first, d)
            opening.append((s, p, d))
    opening.sort(key=lambda o: (o[1] == u) != (o[2] == 1))
    start = [o[0] for o in opening]

    def wide(a, p):
        result = []
        for d in (1, -1):
            names["w", a, p, d], s = send("w", a, 0, p, second, d)
            result.append(s)
        return result

    widest = [s for p in pieces for s in wide(0, p)]
    names["far", u], far_u = send("g", -1, 0, u, first, 1)
    plan.task(f"{first}f-1{u}", [names["f", u, 1]], sends=[far_u] + wide(-1, u))
    names["far", v], far_v = send("g", 1, 0, v, first, -1)
    plan.task(f"{first}f1{v}", [names["f", v, -1]], sends=[far_v] + wide(1, v))
    plan.task(f"{first}f-1{v}", [names["f", v, 1]], sends=wide(-1, v))
    plan.task(f"{first}f1{u}", [names["f", u, -1]], sends=wide(1, u))
    for p in pieces:
        plan.task(f"{first}g{p}", [names["far", p]], sends=wide(2, p))
    for a in (0, -1, 1, 2):
        for p, b, d in ((u, -1, 1), (v, 1, -1)):
            _, s = send("l", a, b, p, second, d)
            plan.task(f"{first}l{a}{p}", [names["w", a, p, d]], sends=[s])
    return start, widest, brings


def plan_passage_gather(plan, pb, quarter):
    z_size = plan.place.z_size
    reach = z_size // 2
    carried = {1: (0, 1), -1: (2, 3)}
    names = []
    start = []

    def ref(offset, p):
        return pb.at[slot_of(offset, z_size), 0, pl.ds(p * quarter, quarter)]

    def push(step, p, d):
        both = lambda: (ref(-d * step, p), ref(-d * (step + 1), p))
        return (f"pg_{step + 1}{p}{d}", "z", d, 32, 0, both)

    def hand_over(offset):
        s = slot_of(offset, z_size)
        names.append(f"pg_c{s}")
        return (f"pg_c{s}", "c", 1, 128, 0, lambda: (pb.at[s, 0], pb.at[s, 1]))

    for d in (1, -1):
        for p in carried[d] + carried[-d]:
            start.append(push(0, p, d))
    for step in range(1, reach):
        for d in (1, -1):
            for p in carried[d] + carried[-d]:
                sends = []
                if step < reach - 1 or p in carried[d]:
                    sends.append(push(step, p, d))
                plan.task(f"z{step}{p}{d}", [f"pg_{step}{p}{d}"], sends=sends)
            plan.task(
                f"h{step}{d}",
                [f"pg_{step}{p}{d}" for p in range(4)],
                sends=[hand_over(-d * step)],
            )
    plan.task(
        f"h{reach}",
        [f"pg_{reach}{p}{d}" for d in (1, -1) for p in carried[d]],
        sends=[hand_over(reach)],
    )
    start.append(hand_over(0))
    return start, names


def plan_plane_scatter(plan, total, landing, late, first, second, ready):
    place = plan.place
    half = total.shape[2] // 2
    parts = (pl.ds(0, half), pl.ds(half, half))
    kib = 64

    def ref(a, b, h=None):
        at = {first: place.at(first, a), second: place.at(second, b)}
        if h is None:
            return total.at[at["x"], at["y"]]
        return total.at[at["x"], at["y"], parts[h]]

    def send(kind, a, b, h, axis, d, dst):
        name = f"rs_{first}{kind}{b}{h}{d}"
        return (name, axis, d, kib, 1, lambda: (ref(a, b, h), dst()))

    def far(k):
        return [
            send("f", 2, k, h, first, d, lambda h=h: landing.at[0, k % RING, parts[h]])
            for h, d in ((0, 1), (1, -1))
        ]

    def own(k):
        return [
            send("n", d, k, h, first, d, lambda h=h, d=d: landing.at[1 if d == 1 else 2, k % RING, parts[h]])
            for h, d in ((1, 1), (0, -1))
        ]

    def acc(k, more, needs=()):
        def run():
            for h, d in ((0, 1), (1, -1)):
                ref(d, k, h)[...] += landing[0, k % RING, parts[h]]

        sends = [
            send("n", d, k, h, first, d, lambda h=h, d=d: landing.at[1 if d == 1 else 2, k % RING, parts[h]])
            for h, d in ((0, 1), (1, -1))
        ]
        needs = [f"rs_{first}f{k}{h}{d}" for h, d in ((0, 1), (1, -1))] + list(needs)
        plan.task(f"{first}acc{k}", needs, run, sends + more, cost=0.15)

    plan.task(f"{first}far2", [ready(2, 2)], sends=far(2))
    plan.task(f"{first}own2", [ready(1, 2), ready(-1, 2)], sends=own(2))
    plan.task(f"{first}far1", [ready(2, 1)], sends=far(1))
    everything = [ready(a, b) for a in (0, 1, 2, -1) for b in (0, 1, 2, -1)]
    acc(2, own(1) + far(-1), everything)
    acc(1, own(-1) + far(0))
    acc(-1, own(0))
    acc(0, [])

    def done(k, sends):
        def run():
            ref(0, k)[...] += landing[1, k % RING] + landing[2, k % RING]

        needs = [f"rs_{first}n{k}{h}{d}" for h in (0, 1) for d in (1, -1)]
        plan.task(f"{first}done{k}", needs, run, sends, cost=0.1)

    def hop(kind, b, h, d, slot):
        return send(kind, 0, b, h, second, d, lambda: late.at[slot, parts[h]])

    done(2, [hop("s", 2, 0, 1, 0), hop("s", 2, 1, -1, 0)])
    done(1, [hop("s", 1, 1, 1, 1)])
    done(-1, [hop("s", -1, 0, -1, 2)])
    done(0, [])
    for d, h, slot in ((1, 0, 1), (-1, 1, 2)):

        def run(d=d, h=h):
            ref(0, d, h)[...] += late[0, parts[h]]

        plan.task(
            f"{first}turn{d}",
            [f"rs_{first}s2{h}{d}", f"{first}done{d}"],
            run,
            [hop("t", d, h, d, slot)],
            cost=0.1,
        )
    last = [f"rs_{first}s11{1}", f"rs_{first}s-10{-1}", f"rs_{first}t10{1}", f"rs_{first}t-11{-1}"]
    return last + [f"{first}done0"]


def plan_line_scatter(plan, total, across, landing, rows, ready):
    z_size = plan.place.z_size
    reach = z_size // 2
    half = rows // 2
    parts = (pl.ds(0, half), pl.ds(half, half))

    def settle(k):
        s = slot_of(k, z_size)
        total[s, 0] += across[s]

    def push(d, h, step):
        s = slot_of(d * (reach - step), z_size)
        both = lambda: (total.at[s, 0, parts[h]], landing.at[0 if d == 1 else 1, step, parts[h]])
        return (f"rz_{d}{h}{step}", "z", d, 128, 2, both)

    for k in [reach] + [s for k in range(reach - 1, 0, -1) for s in (k, -k)] + [0]:
        s = slot_of(k, z_size)
        gift = (f"rz_c{s}", "c", 1, 256, 2, lambda s=s: (total.at[s, 1], across.at[s]))
        plan.task(f"gift{s}", [ready(s)], sends=[gift])
        sends = []
        if k == reach:
            sends = [push(1, 0, 0), push(-1, 1, 0)]
        elif k == reach - 1:
            sends = [push(1, 1, 1)]
        elif k == 1 - reach:
            sends = [push(-1, 0, 1)]
        plan.task(f"settle{s}", [f"rz_c{s}", f"gift{s}"], lambda k=k: settle(k), sends, cost=0.12)
    for step in range(1, reach):
        for d in (1, -1):
            for h in (0, 1):
                full = (d == 1) == (h == 0)
                if not full and step == 1:
                    continue
                s = slot_of(d * (reach - step), z_size)

                def run(d=d, h=h, s=s, step=step):
                    total[s, 0, parts[h]] += landing[0 if d == 1 else 1, step - 1, parts[h]]

                plan.task(
                    f"rz{d}{h}{step}",
                    [f"rz_{d}{h}{step - 1}", f"settle{s}"],
                    run,
                    [push(d, h, step)],
                    cost=0.1,
                )
    return [f"rz_{d}{h}{reach - 1}" for d in (1, -1) for h in (0, 1)] + ["settle0"]


def kernel(
    zl_size,
    z_size,
    q_in,
    p_in,
    t_in,
    loss_out,
    qg_out,
    pg_out,
    qb,
    pb,
    tb,
    scores,
    weights,
    stats,
    stats_x,
    mid,
    stats_y,
    factor,
    qga,
    qgb,
    pg,
    land_a,
    land_b,
    late_a,
    late_b,
    across,
    land_z,
    send_sem,
    recv_sem,
):
    rows, width = q_in.shape
    quarter = rows // 4
    group = RING * rows
    columns = 2 * z_size * rows
    place = Place(zl_size, z_size)
    peers = [("x", k) for k in (1, 2, 3)] + [("y", k) for k in (1, 2, 3)]
    peers += [("z", 1), ("z", z_size - 1), ("c", 1)]
    barrier = pltpu.get_barrier_semaphore()
    for axis, k in peers:
        pl.semaphore_signal(
            barrier,
            inc=1,
            device_id=place.device(axis, k),
            device_id_type=pl.DeviceIdType.MESH,
        )
    qb[place.x, place.y] = q_in[...].astype(jnp.bfloat16)
    pb[0, 0] = p_in[...].astype(jnp.bfloat16)
    mine = t_in[...]
    tb[place.x * RING + place.y] = jnp.broadcast_to(
        jnp.concatenate([mine] * (128 // rows), axis=1), (8, 128)
    )
    pl.semaphore_wait(barrier, len(peers))

    plan = Plan(place, recv_sem, send_sem)

    start_a, wide_a, brings_a = plan_query_gather(plan, qb, "x", "y", (0, 1), quarter)
    start_b, wide_b, brings_b = plan_query_gather(plan, qb, "y", "x", (2, 3), quarter)
    start_p, crossing = plan_passage_gather(plan, pb, quarter)

    def tile():
        return (tb.at[place.x * RING + place.y],) * 2

    def tiles():
        return (tb.at[pl.ds(place.x * RING, RING)],) * 2

    ty = [(f"tg_y{k}", "y", k, 4, 3, tile) for k in (1, 2, 3)]
    tx = [(f"tg_x{k}", "x", k, 16, 3, tiles) for k in (1, 2, 3)]
    plan.task("open", sends=start_p + start_a + start_b + ty + wide_a + wide_b, rank=-1)
    plan.task("ty", [s[0] for s in ty], sends=tx)

    def at_x(a):
        return place.at("x", a)

    def spot(a):
        return pl.ds(pl.multiple_of(at_x(a) * columns, columns), columns)

    def multiply(a, h):
        size = columns // 2
        some = pb[h * z_size // 2 : (h + 1) * z_size // 2].reshape(size, width)
        queries = qb[at_x(a)].reshape(group, width)
        start = pl.multiple_of(at_x(a) * columns + h * size, size)
        scores[pl.ds(start, size)] = (
            lax.dot_general(
                some, queries, (((1,), (1,)), ((), ())), preferred_element_type=jnp.float32
            )
            * logit_scale
        )

    band = 128
    bands = columns // band

    def target_of(a):
        line = at_x(a) * RING
        value = jnp.concatenate([tb[line + ys, 0:1, 0:rows] for ys in range(RING)], axis=1)
        inside = lax.rem(value, rows)
        value = lax.div(value, rows)
        zh_size = z_size // zl_size
        zh = lax.rem(value, zh_size)
        value = lax.div(value, zh_size)
        core = lax.rem(value, 2)
        value = lax.div(value, 2)
        y = lax.rem(value, RING)
        value = lax.div(value, RING)
        zl = lax.rem(value, zl_size)
        x = lax.div(value, zl_size)
        apart = lax.rem(zh * zl_size + zl - place.z + z_size, z_size)
        slot = jnp.where(apart == 0, 0, jnp.where(apart <= z_size // 2, 2 * apart - 1, 2 * (z_size - apart)))
        local = (slot * 2 + lax.rem(core + place.c, 2)) * rows + inside
        return jnp.where((x == place.x) & (y == place.y), local, -1)

    def fold(value, how):
        return how(value.reshape(band // 8, 8, group), axis=0)

    def piece_of(a, b):
        return pl.ds(pl.multiple_of(at_x(a) * columns + b * band, band), band)

    def measure(a):
        target = target_of(a)

        def top(b, highest):
            return jnp.maximum(highest, fold(scores[piece_of(a, b)], jnp.max))

        highest = lax.fori_loop(0, bands, top, jnp.full((8, group), -jnp.inf, jnp.float32))
        highest = jnp.max(highest, axis=0, keepdims=True)

        def terms(b, totals):
            value = scores[piece_of(a, b)]
            spots = lax.broadcasted_iota(jnp.int32, (band, group), 0) + b * band
            hit = jnp.where(spots == target, value, 0.0)
            value = jnp.exp(value - highest)
            scores[piece_of(a, b)] = value
            return totals[0] + fold(value, jnp.sum), totals[1] + fold(hit, jnp.sum)

        zero = jnp.zeros((8, group), jnp.float32)
        total, hit = lax.fori_loop(0, bands, terms, (zero, zero))
        for k, value in enumerate(
            (highest, jnp.sum(total, axis=0, keepdims=True), jnp.sum(hit, axis=0, keepdims=True))
        ):
            stats[pl.ds(k * RING + at_x(a), 1)] = value

    near_half = [f"pg_c{s}" for s in range(z_size // 2)]
    for s in range(1, z_size // 2):
        k = (s + 1) // 2 * (1 if s % 2 else -1)
        near_half.append(f"h{abs(k)}{-1 if k > 0 else 1}")
    whole = [t[0] for t in plan.tasks if t[0].startswith("h")]
    for rank, a in enumerate((0, -1, 1, 2)):
        needs = [n for b in (-1, 0, 1, 2) for n in brings_a.get((a, b), []) + brings_b.get((b, a), [])]
        plan.task(f"mul{a}0", needs + near_half, lambda a=a: multiply(a, 0), cost=0.45, rank=1 + rank)
        plan.task(
            f"mul{a}1",
            [f"mul{a}0"] + whole + crossing,
            lambda a=a: multiply(a, 1),
            cost=0.45,
            rank=1 + rank,
        )
        plan.task(
            f"measure{a}",
            [f"mul{a}1"] + [s[0] for s in tx],
            lambda a=a: measure(a),
            cost=0.5,
            rank=1 + rank,
        )

    def combined(own, others):
        pieces = [own[...]] + [others[k] for k in range(3)]
        tops = [piece[:RING] for piece in pieces]
        highest = functools.reduce(jnp.maximum, tops)
        total = sum(
            piece[RING : 2 * RING] * jnp.exp(top - highest) for piece, top in zip(pieces, tops)
        )
        positive = sum(piece[2 * RING : 3 * RING] for piece in pieces)
        return highest, total, positive

    def half_way():
        highest, total, positive = combined(stats, stats_x)
        mid[0:RING] = highest
        mid[RING : 2 * RING] = total
        mid[2 * RING : 3 * RING] = positive

    def normalise():
        highest, total, positive = combined(mid, stats_y)
        log_norm = highest + jnp.log(total)
        losses = log_norm - positive
        line = lax.broadcasted_iota(jnp.int32, losses.shape, 0)
        losses = jnp.sum(jnp.where(line == place.x, losses, 0.0), axis=0, keepdims=True)
        picked = losses[:, :rows]
        for ys in range(1, RING):
            picked = jnp.where(place.y == ys, losses[:, ys * rows : (ys + 1) * rows], picked)
        loss_out[...] = picked
        factor[0:RING] = jnp.exp(stats[0:RING] - log_norm)

    def blank():
        stats[3 * RING :] = jnp.zeros((RING, group), jnp.float32)
        mid[3 * RING :] = jnp.zeros((RING, group), jnp.float32)
        factor[RING:] = jnp.zeros((RING, group), jnp.float32)

    plan.task("blank", run=blank)
    sx = [(f"st_x{k}", "x", k, 16, 0, lambda k=k: (stats, stats_x.at[k - 1])) for k in (1, 2, 3)]
    sy = [(f"st_y{k}", "y", k, 16, 0, lambda k=k: (mid, stats_y.at[k - 1])) for k in (1, 2, 3)]
    everything = [t[0] for t in plan.tasks]
    plan.task("sx", everything, sends=sx)
    plan.task("half", [s[0] for s in sx], half_way, sy)
    plan.task("norm", [s[0] for s in sy], normalise)

    def weigh(a):
        target = target_of(a)
        scale = factor[pl.ds(at_x(a), 1)]
        lanes = pl.ds(pl.multiple_of(at_x(a) * group, group), group)

        def step(b, carry):
            spots = lax.broadcasted_iota(jnp.int32, (band, group), 0) + b * band
            onehot = jnp.where(spots == target, 1.0, 0.0)
            weights[pl.ds(pl.multiple_of(b * band, band), band), lanes] = (
                (scores[piece_of(a, b)] * scale - onehot) * logit_scale
            ).astype(jnp.bfloat16)
            return carry

        lax.fori_loop(0, bands, step, 0)

    def passage_terms(first, last):
        some = weights[first * 2 * rows : last * 2 * rows]
        queries = qb[...].reshape(RING * group, width)
        pg[first:last] = jnp.dot(some, queries, preferred_element_type=jnp.float32).reshape(
            last - first, 2, rows, width
        )

    def query_terms(a):
        some = weights[:, pl.ds(pl.multiple_of(at_x(a) * group, group), group)]
        part = lax.dot_general(
            some,
            pb[...].reshape(columns, width),
            (((0,), (0,)), ((), ())),
            preferred_element_type=jnp.float32,
        )
        qga[at_x(a)] = part[:, : width // 2].reshape(RING, rows, width // 2)
        qgb[at_x(a)] = part[:, width // 2 :].reshape(RING, rows, width // 2)

    def all_weights():
        for a in (2, 1, -1, 0):
            weigh(a)

    cut = z_size - 3
    plan.task("weights", ["norm"], all_weights, cost=0.5)
    plan.task("pterms0", ["weights"], lambda: passage_terms(cut, z_size), cost=0.8)
    plan.task("qterms2", ["pterms0"], lambda: query_terms(2), cost=0.8, rank=1)
    plan.task("qterms1", ["qterms2"], lambda: query_terms(1), cost=0.8, rank=2)
    plan.task("qterms-1", ["qterms1"], lambda: query_terms(-1), cost=0.8, rank=2)
    plan.task("pterms1", ["qterms-1"], lambda: passage_terms(0, cut), cost=1.2, rank=3)
    plan.task("qterms0", ["pterms1"], lambda: query_terms(0), cost=0.8, rank=4)

    def chunk(a):
        return f"qterms{(a + 1) % 4 - 1}"

    end_a = plan_plane_scatter(plan, qga, land_a, late_a, "x", "y", lambda a, b: chunk(a))
    end_b = plan_plane_scatter(plan, qgb, land_b, late_b, "y", "x", lambda a, b: chunk(b))
    end_p = plan_line_scatter(
        plan, pg, across, land_z, rows, lambda s: "pterms0" if s >= cut else "pterms1"
    )

    def out_a():
        qg_out[:, : width // 2] = qga[place.x, place.y] + late_a[1] + late_a[2]

    def out_b():
        qg_out[:, width // 2 :] = qgb[place.x, place.y] + late_b[1] + late_b[2]

    def out_p():
        last = z_size // 2 - 1
        pg_out[...] = pg[0, 0] + (land_z[0, last] + land_z[1, last])

    plan.task("out_a", end_a, out_a)
    plan.task("out_b", end_b, out_b)
    plan.task("out_p", end_p, out_p)
    plan.run()
    plan.finish(scores, 0)
    plan.finish(scores, 1)
    plan.finish(scores, 2)
    plan.finish(tb, 3, per_kib=4)


def put_out(*refs):
    for source, target in zip(refs[:3], refs[3:]):
        target[...] = source[...]


def body(zl_size, z_size, queries, passages, positives):
    rows, width = queries.shape
    group = RING * rows
    columns = 2 * z_size * rows
    f32, bf16 = jnp.float32, jnp.bfloat16
    reach = z_size // 2
    shapes = (
        jax.ShapeDtypeStruct((1, rows), f32),
        jax.ShapeDtypeStruct((rows, width), f32),
        jax.ShapeDtypeStruct((rows, width), f32),
    )
    landing = pltpu.VMEM((3, RING, rows, width // 2), f32)
    results = pl.pallas_call(
        functools.partial(kernel, zl_size, z_size),
        out_shape=shapes,
        in_specs=[pl.BlockSpec(memory_space=pltpu.VMEM)] * 3,
        out_specs=[pl.BlockSpec(memory_space=pltpu.VMEM)] * 3,
        scratch_shapes=[
            pltpu.VMEM((RING, RING, rows, width), bf16),
            pltpu.VMEM((z_size, 2, rows, width), bf16),
            pltpu.VMEM((RING * RING, 8, 128), jnp.int32),
            pltpu.VMEM((RING * columns, group), f32),
            pltpu.VMEM((columns, RING * group), bf16),
            pltpu.VMEM((4 * RING, group), f32),
            pltpu.VMEM((3, 4 * RING, group), f32),
            pltpu.VMEM((4 * RING, group), f32),
            pltpu.VMEM((3, 4 * RING, group), f32),
            pltpu.VMEM((2 * RING, group), f32),
            pltpu.VMEM((RING, RING, rows, width // 2), f32),
            pltpu.VMEM((RING, RING, rows, width // 2), f32),
            pltpu.VMEM((z_size, 2, rows, width), f32),
            landing,
            landing,
            pltpu.VMEM((3, rows, width // 2), f32),
            pltpu.VMEM((3, rows, width // 2), f32),
            pltpu.VMEM((z_size, rows, width), f32),
            pltpu.VMEM((2, reach, rows, width), f32),
            pltpu.SemaphoreType.DMA((4,)),
            pltpu.SemaphoreType.DMA((SIGNALS,)),
        ],
        compiler_params=pltpu.CompilerParams(
            collective_id=0, has_side_effects=True, vmem_limit_bytes=56 * 1024 * 1024
        ),
    )(queries, passages, positives.reshape(1, rows))
    losses, query_grads, passage_grads = pl.pallas_call(
        put_out,
        out_shape=shapes,
        in_specs=[pl.BlockSpec(memory_space=pltpu.VMEM)] * 3,
        out_specs=[pl.BlockSpec(memory_space=pltpu.VMEM)] * 3,
    )(*results)
    return losses.reshape(rows), query_grads, passage_grads


def solution(mesh):
    zl_size, z_hi = 2, mesh.shape["sub"]
    torus = Mesh(mesh.devices.reshape(RING, zl_size, RING, 2, z_hi), AXES)
    return jax.shard_map(
        functools.partial(body, zl_size, zl_size * z_hi),
        mesh=torus,
        in_specs=(P(AXES, None), P(AXES, None), P(AXES)),
        out_specs=(P(AXES), P(AXES, None), P(AXES, None)),
        check_vma=False,
    )
```

time: 402 us -> 70.5 us (0.18)
  the two profiles are of different devices: /device:TPU:64 before, /device:TPU:1 now
where the time goes in v2:
time: 70.5 us; the launch traced here: 70.3 us
  Pallas kernels  69.7 us (99%)
    pallas_call x1, Pallas kernels, body(): pl.pallas_call(functools.partial(kernel, zl_size, z_size), out_shape=shap...  67.9 us
    pallas_call x1, Pallas kernels, body(): pl.pallas_call(put_out, out_shape=shapes, in_specs=[pl.BlockSpec(memory_s...  1.85 us

profile of v2, /device:TPU:1, one launch (start us, length us, event | category | flops | bytes accessed | tf_op | source)
XLA Modules:
  0.0 70.3 jit_solution(13867469007466000370)
XLA Ops:
  0.6 67.9 %shard_map.58 = (f32[1,64]{1,0:T(1,128)}, f32[64,1024]{1,0:T(8,128)}, f32[64,1024]{1,0:T(8,128)}) custom-call(f32[64,1024]{1,0:T(8,128)} %q_in.1, f32[64,1024]{1,0:T(8,128)} %p_in.1, s32[1,64]{1,0:T(1,128)} %bitcast.2), custom_call_target="tpu_custom_call" | custom-call | tf_op jit(solution)/shard_map/pallas_call | solution.py:640
  68.5 1.8 %shard_map.59 = (f32[1,64]{1,0:T(1,128)}, f32[64,1024]{1,0:T(8,128)}, f32[64,1024]{1,0:T(8,128)}) custom-call(f32[1,64]{1,0:T(1,128)} %get-tuple-element.9.refs_0_, f32[64,1024]{1,0:T(8,128)} %get-tuple-element.10.refs_1_, f32[64,1024]{1,0:T(8,128)} %get-tuple-element.11.refs_2_), custom_call_target="tpu_custom_call" | custom-call | tf_op jit(solution)/shard_map/pallas_call | solution.py:672

commit v3 on v2

--- a/solution.py
+++ b/solution.py
@@ -11,10 +11,10 @@
 AXES = ("x", "zl", "y", "c", "zh")
 RING = 4
 logit_scale = 20.0
-SIGNALS = 136
+SIGNALS = 144
 
 WIRE = {"x": 0.022, "y": 0.022, "z": 0.022, "c": 0.0016}
-DELAY = {"x": 2.4, "y": 2.4, "z": 2.5, "c": 1.0}
+DELAY = {"x": 2.6, "y": 2.6, "z": 2.6, "c": 0.9}
 
 
 class Place:
@@ -59,9 +59,15 @@
             now = max(now, start) + task[4]
             known[task[0]] = now
             for message, axis, offset, kib, _, _ in task[3]:
-                lane = (axis, offset)
-                link[lane] = max(link.get(lane, 0.0), now) + kib * WIRE[axis]
-                known[message] = link[lane] + DELAY[axis]
+                if axis in "xy" and offset == 2:
+                    for lane in ((axis, 1), (axis, -1)):
+                        link[lane] = max(link.get(lane, 0.0), now) + kib * WIRE[axis]
+                    known[message] = max(link[axis, 1], link[axis, -1]) + DELAY[axis] + 0.6
+                    continue
+                far = abs(offset)
+                lane = (axis, offset // far)
+                link[lane] = max(link.get(lane, 0.0), now) + kib * WIRE[axis] * far
+                known[message] = link[lane] + DELAY[axis] + 0.5 * (far - 1)
             waiting = [w for w in waiting if w[0] != index]
             result.append(task)
         return result
@@ -112,6 +118,12 @@
         ).wait_send()
 
 
+def unrolled(first, last, step, carry):
+    for k in range(first, last):
+        carry = step(k, carry)
+    return carry
+
+
 def slot_of(offset, z_size):
     offset = offset % z_size
     if offset == 0:
@@ -155,12 +167,12 @@
         return result
 
     widest = [s for p in pieces for s in wide(0, p)]
-    names["far", u], far_u = send("g", -1, 0, u, first, 1)
-    plan.task(f"{first}f-1{u}", [names["f", u, 1]], sends=[far_u] + wide(-1, u))
-    names["far", v], far_v = send("g", 1, 0, v, first, -1)
-    plan.task(f"{first}f1{v}", [names["f", v, -1]], sends=[far_v] + wide(1, v))
-    plan.task(f"{first}f-1{v}", [names["f", v, 1]], sends=wide(-1, v))
-    plan.task(f"{first}f1{u}", [names["f", u, -1]], sends=wide(1, u))
+    for p in pieces:
+        names["far", p], s = send("g", 0, 0, p, first, 2)
+        widest.append(s)
+    for p in pieces:
+        plan.task(f"{first}f-1{p}", [names["f", p, 1]], sends=wide(-1, p))
+        plan.task(f"{first}f1{p}", [names["f", p, -1]], sends=wide(1, p))
     for p in pieces:
         plan.task(f"{first}g{p}", [names["far", p]], sends=wide(2, p))
     for a in (0, -1, 1, 2):
@@ -180,9 +192,9 @@
     def ref(offset, p):
         return pb.at[slot_of(offset, z_size), 0, pl.ds(p * quarter, quarter)]
 
-    def push(step, p, d):
-        both = lambda: (ref(-d * step, p), ref(-d * (step + 1), p))
-        return (f"pg_{step + 1}{p}{d}", "z", d, 32, 0, both)
+    def push(step, p, d, places=1):
+        both = lambda: (ref(-d * step, p), ref(-d * (step + places), p))
+        return (f"pg_{step + places}{p}{d}", "z", d * places, 32, 0, both)
 
     def hand_over(offset):
         s = slot_of(offset, z_size)
@@ -196,7 +208,9 @@
         for d in (1, -1):
             for p in carried[d] + carried[-d]:
                 sends = []
-                if step < reach - 1 or p in carried[d]:
+                if step == reach - 2 and p in carried[d]:
+                    sends.append(push(step, p, d, 2))
+                if step < reach - 1:
                     sends.append(push(step, p, d))
                 plan.task(f"z{step}{p}{d}", [f"pg_{step}{p}{d}"], sends=sends)
             plan.task(
@@ -213,41 +227,44 @@
     return start, names
 
 
-def plan_plane_scatter(plan, total, landing, late, first, second, ready):
+def plan_plane_scatter(plan, total, short, landing, late, first, second, ready):
     place = plan.place
     half = total.shape[2] // 2
     parts = (pl.ds(0, half), pl.ds(half, half))
-    kib = 64
-
-    def ref(a, b, h=None):
+    far_land, near_land, sum_land = landing
+
+    def view(array, a, b, h=None):
         at = {first: place.at(first, a), second: place.at(second, b)}
         if h is None:
-            return total.at[at["x"], at["y"]]
-        return total.at[at["x"], at["y"], parts[h]]
-
-    def send(kind, a, b, h, axis, d, dst):
+            return array.at[at["x"], at["y"]]
+        return array.at[at["x"], at["y"], parts[h]]
+
+    def ref(a, b, h=None):
+        return view(total, a, b, h)
+
+    def send(kind, a, b, h, axis, d, dst, array=total, kib=64):
         name = f"rs_{first}{kind}{b}{h}{d}"
-        return (name, axis, d, kib, 1, lambda: (ref(a, b, h), dst()))
+        return (name, axis, d, kib, 1, lambda: (view(array, a, b, h), dst()))
 
     def far(k):
         return [
-            send("f", 2, k, h, first, d, lambda h=h: landing.at[0, k % RING, parts[h]])
+            send("f", 2, k, h, first, d, lambda h=h: far_land.at[k % RING, parts[h]], short, 32)
             for h, d in ((0, 1), (1, -1))
         ]
 
     def own(k):
         return [
-            send("n", d, k, h, first, d, lambda h=h, d=d: landing.at[1 if d == 1 else 2, k % RING, parts[h]])
+            send("n", d, k, h, first, d, lambda h=h: near_land.at[k % RING, parts[h]], short, 32)
             for h, d in ((1, 1), (0, -1))
         ]
 
     def acc(k, more, needs=()):
         def run():
             for h, d in ((0, 1), (1, -1)):
-                ref(d, k, h)[...] += landing[0, k % RING, parts[h]]
+                ref(d, k, h)[...] += far_land[k % RING, parts[h]].astype(jnp.float32)
 
         sends = [
-            send("n", d, k, h, first, d, lambda h=h, d=d: landing.at[1 if d == 1 else 2, k % RING, parts[h]])
+            send("n", d, k, h, first, d, lambda h=h: sum_land.at[k % RING, parts[h]])
             for h, d in ((0, 1), (1, -1))
         ]
         needs = [f"rs_{first}f{k}{h}{d}" for h, d in ((0, 1), (1, -1))] + list(needs)
@@ -264,7 +281,7 @@
 
     def done(k, sends):
         def run():
-            ref(0, k)[...] += landing[1, k % RING] + landing[2, k % RING]
+            ref(0, k)[...] += near_land[k % RING].astype(jnp.float32) + sum_land[k % RING]
 
         needs = [f"rs_{first}n{k}{h}{d}" for h in (0, 1) for d in (1, -1)]
         plan.task(f"{first}done{k}", needs, run, sends, cost=0.1)
@@ -292,20 +309,34 @@
     return last + [f"{first}done0"]
 
 
-def plan_line_scatter(plan, total, across, landing, rows, ready):
+def plan_line_scatter(plan, total, across, short, short_land, landing, rows, ready):
     z_size = plan.place.z_size
     reach = z_size // 2
-    half = rows // 2
-    parts = (pl.ds(0, half), pl.ds(half, half))
+    quarter = rows // 4
+    parts = [pl.ds(k * quarter, quarter) for k in range(4)]
+    carried = {1: (0, 1), -1: (2, 3)}
+    opening = {reach: 0, reach - 1: 1, 1 - reach: 2}
+
+    def opens(d, q):
+        return 0 if q in carried[d] else 1
 
     def settle(k):
         s = slot_of(k, z_size)
         total[s, 0] += across[s]
-
-    def push(d, h, step):
-        s = slot_of(d * (reach - step), z_size)
-        both = lambda: (total.at[s, 0, parts[h]], landing.at[0 if d == 1 else 1, step, parts[h]])
-        return (f"rz_{d}{h}{step}", "z", d, 128, 2, both)
+        if k in opening:
+            short[opening[k]] = total[s, 0].astype(jnp.bfloat16)
+
+    def push(d, q, step):
+        k = d * (reach - step)
+        s = slot_of(k, z_size)
+        lane = 0 if d == 1 else 1
+        name = f"rz_{d}{q}{step}"
+        if step == opens(d, q):
+            number = opening[k if step else reach]
+            both = lambda: (short.at[number, parts[q]], short_land.at[lane, parts[q]])
+            return (name, "z", d, 32, 2, both)
+        both = lambda: (total.at[s, 0, parts[q]], landing.at[lane, step - 1, parts[q]])
+        return (name, "z", d, 64, 2, both)
 
     for k in [reach] + [s for k in range(reach - 1, 0, -1) for s in (k, -k)] + [0]:
         s = slot_of(k, z_size)
@@ -313,31 +344,35 @@
         plan.task(f"gift{s}", [ready(s)], sends=[gift])
         sends = []
         if k == reach:
-            sends = [push(1, 0, 0), push(-1, 1, 0)]
+            sends = [push(d, q, 0) for d in (1, -1) for q in carried[d]]
         elif k == reach - 1:
-            sends = [push(1, 1, 1)]
+            sends = [push(1, q, 1) for q in carried[-1]]
         elif k == 1 - reach:
-            sends = [push(-1, 0, 1)]
+            sends = [push(-1, q, 1) for q in carried[1]]
         plan.task(f"settle{s}", [f"rz_c{s}", f"gift{s}"], lambda k=k: settle(k), sends, cost=0.12)
     for step in range(1, reach):
         for d in (1, -1):
-            for h in (0, 1):
-                full = (d == 1) == (h == 0)
-                if not full and step == 1:
+            for q in carried[d] + carried[-d]:
+                if step <= opens(d, q):
                     continue
                 s = slot_of(d * (reach - step), z_size)
 
-                def run(d=d, h=h, s=s, step=step):
-                    total[s, 0, parts[h]] += landing[0 if d == 1 else 1, step - 1, parts[h]]
+                def run(d=d, q=q, s=s, step=step):
+                    lane = 0 if d == 1 else 1
+                    if step - 1 == opens(d, q):
+                        value = short_land[lane, parts[q]].astype(jnp.float32)
+                    else:
+                        value = landing[lane, step - 2, parts[q]]
+                    total[s, 0, parts[q]] += value
 
                 plan.task(
-                    f"rz{d}{h}{step}",
-                    [f"rz_{d}{h}{step - 1}", f"settle{s}"],
+                    f"rz{d}{q}{step}",
+                    [f"rz_{d}{q}{step - 1}", f"settle{s}"],
                     run,
-                    [push(d, h, step)],
-                    cost=0.1,
+                    [push(d, q, step)],
+                    cost=0.06,
                 )
-    return [f"rz_{d}{h}{reach - 1}" for d in (1, -1) for h in (0, 1)] + ["settle0"]
+    return [f"rz_{d}{q}{reach - 1}" for d in (1, -1) for q in range(4)] + ["settle0"]
 
 
 def kernel(
@@ -354,6 +389,10 @@
     tb,
     scores,
     weights,
+    targets,
+    tops,
+    sums,
+    hits,
     stats,
     stats_x,
     mid,
@@ -361,12 +400,20 @@
     factor,
     qga,
     qgb,
+    qsa,
+    qsb,
     pg,
-    land_a,
-    land_b,
+    far_a,
+    near_a,
+    sum_a,
+    far_b,
+    near_b,
+    sum_b,
     late_a,
     late_b,
     across,
+    short_z,
+    short_land_z,
     land_z,
     send_sem,
     recv_sem,
@@ -377,7 +424,7 @@
     columns = 2 * z_size * rows
     place = Place(zl_size, z_size)
     peers = [("x", k) for k in (1, 2, 3)] + [("y", k) for k in (1, 2, 3)]
-    peers += [("z", 1), ("z", z_size - 1), ("c", 1)]
+    peers += [("z", k) for k in (1, 2, z_size - 2, z_size - 1)] + [("c", 1)]
     barrier = pltpu.get_barrier_semaphore()
     for axis, k in peers:
         pl.semaphore_signal(
@@ -414,17 +461,19 @@
     def at_x(a):
         return place.at("x", a)
 
-    def spot(a):
-        return pl.ds(pl.multiple_of(at_x(a) * columns, columns), columns)
-
-    def multiply(a, h):
-        size = columns // 2
-        some = pb[h * z_size // 2 : (h + 1) * z_size // 2].reshape(size, width)
+    groups = ((0, z_size // 2), (z_size // 2, z_size - 1), (z_size - 1, z_size))
+
+    def multiply(a, g):
+        first, last = groups[g]
+        size = (last - first) * 2 * rows
         queries = qb[at_x(a)].reshape(group, width)
-        start = pl.multiple_of(at_x(a) * columns + h * size, size)
+        start = pl.multiple_of(at_x(a) * columns + first * 2 * rows, 2 * rows)
         scores[pl.ds(start, size)] = (
             lax.dot_general(
-                some, queries, (((1,), (1,)), ((), ())), preferred_element_type=jnp.float32
+                pb[first:last].reshape(size, width),
+                queries,
+                (((1,), (1,)), ((), ())),
+                preferred_element_type=jnp.float32,
             )
             * logit_scale
         )
@@ -432,24 +481,32 @@
     band = 128
     bands = columns // band
 
-    def target_of(a):
-        line = at_x(a) * RING
-        value = jnp.concatenate([tb[line + ys, 0:1, 0:rows] for ys in range(RING)], axis=1)
-        inside = lax.rem(value, rows)
-        value = lax.div(value, rows)
-        zh_size = z_size // zl_size
-        zh = lax.rem(value, zh_size)
-        value = lax.div(value, zh_size)
-        core = lax.rem(value, 2)
-        value = lax.div(value, 2)
-        y = lax.rem(value, RING)
-        value = lax.div(value, RING)
-        zl = lax.rem(value, zl_size)
-        x = lax.div(value, zl_size)
-        apart = lax.rem(zh * zl_size + zl - place.z + z_size, z_size)
-        slot = jnp.where(apart == 0, 0, jnp.where(apart <= z_size // 2, 2 * apart - 1, 2 * (z_size - apart)))
-        local = (slot * 2 + lax.rem(core + place.c, 2)) * rows + inside
-        return jnp.where((x == place.x) & (y == place.y), local, -1)
+    def find_targets():
+        def split(value, size):
+            if size & (size - 1):
+                return lax.div(value, size), lax.rem(value, size)
+            return value >> (size.bit_length() - 1), value & (size - 1)
+
+        value = jnp.concatenate(
+            [
+                jnp.concatenate([tb[xs * RING + ys, 0:1, 0:rows] for ys in range(RING)], axis=1)
+                for xs in range(RING)
+            ],
+            axis=0,
+        )
+        value, inside = split(value, rows)
+        value, zh = split(value, z_size // zl_size)
+        value, core = split(value, 2)
+        value, y = split(value, RING)
+        x, zl = split(value, zl_size)
+        apart = zh * zl_size + zl - place.z
+        apart = jnp.where(apart < 0, apart + z_size, apart)
+        slot = jnp.where(apart <= z_size // 2, 2 * apart - 1, 2 * (z_size - apart))
+        slot = jnp.where(apart == 0, 0, slot)
+        local = (slot * 2 + jnp.where(core == place.c, 0, 1)) * rows + inside
+        targets[0:RING] = jnp.where((x == place.x) & (y == place.y), local, -1)
+
+    plan.task("targets", [s[0] for s in tx], find_targets, cost=0.2)
 
     def fold(value, how):
         return how(value.reshape(band // 8, 8, group), axis=0)
@@ -457,13 +514,15 @@
     def piece_of(a, b):
         return pl.ds(pl.multiple_of(at_x(a) * columns + b * band, band), band)
 
-    def measure(a):
-        target = target_of(a)
+    def measure(a, g):
+        multiply(a, g)
+        target = targets[pl.ds(at_x(a), 1)]
+        low, high = (k * 2 * rows // band for k in groups[g])
 
         def top(b, highest):
             return jnp.maximum(highest, fold(scores[piece_of(a, b)], jnp.max))
 
-        highest = lax.fori_loop(0, bands, top, jnp.full((8, group), -jnp.inf, jnp.float32))
+        highest = unrolled(low, high, top, jnp.full((8, group), -jnp.inf, jnp.float32))
         highest = jnp.max(highest, axis=0, keepdims=True)
 
         def terms(b, totals):
@@ -475,79 +534,70 @@
             return totals[0] + fold(value, jnp.sum), totals[1] + fold(hit, jnp.sum)
 
         zero = jnp.zeros((8, group), jnp.float32)
-        total, hit = lax.fori_loop(0, bands, terms, (zero, zero))
-        for k, value in enumerate(
-            (highest, jnp.sum(total, axis=0, keepdims=True), jnp.sum(hit, axis=0, keepdims=True))
-        ):
-            stats[pl.ds(k * RING + at_x(a), 1)] = value
-
-    near_half = [f"pg_c{s}" for s in range(z_size // 2)]
-    for s in range(1, z_size // 2):
+        total, hit = unrolled(low, high, terms, (zero, zero))
+        total = jnp.sum(total, axis=0, keepdims=True)
+        tops[pl.ds(g * RING + at_x(a), 1)] = highest
+        sums[pl.ds(g * RING + at_x(a), 1)] = highest + jnp.log(total)
+        hits[pl.ds(g * RING + at_x(a), 1)] = jnp.sum(hit, axis=0, keepdims=True)
+
+    def arrived(s):
+        if s == 0:
+            return [crossing_of[s]]
+        if s == z_size - 1:
+            return [crossing_of[s], f"h{z_size // 2}"]
         k = (s + 1) // 2 * (1 if s % 2 else -1)
-        near_half.append(f"h{abs(k)}{-1 if k > 0 else 1}")
-    whole = [t[0] for t in plan.tasks if t[0].startswith("h")]
+        return [crossing_of[s], f"h{abs(k)}{-1 if k > 0 else 1}"]
+
+    crossing_of = {int(name[4:]): name for name in crossing}
     for rank, a in enumerate((0, -1, 1, 2)):
         needs = [n for b in (-1, 0, 1, 2) for n in brings_a.get((a, b), []) + brings_b.get((b, a), [])]
-        plan.task(f"mul{a}0", needs + near_half, lambda a=a: multiply(a, 0), cost=0.45, rank=1 + rank)
-        plan.task(
-            f"mul{a}1",
-            [f"mul{a}0"] + whole + crossing,
-            lambda a=a: multiply(a, 1),
-            cost=0.45,
-            rank=1 + rank,
-        )
-        plan.task(
-            f"measure{a}",
-            [f"mul{a}1"] + [s[0] for s in tx],
-            lambda a=a: measure(a),
-            cost=0.5,
-            rank=1 + rank,
-        )
-
-    def combined(own, others):
-        pieces = [own[...]] + [others[k] for k in range(3)]
-        tops = [piece[:RING] for piece in pieces]
-        highest = functools.reduce(jnp.maximum, tops)
-        total = sum(
-            piece[RING : 2 * RING] * jnp.exp(top - highest) for piece, top in zip(pieces, tops)
-        )
-        positive = sum(piece[2 * RING : 3 * RING] for piece in pieces)
-        return highest, total, positive
+        needs += ["targets"]
+        for g, (first, last) in enumerate(groups):
+            plan.task(
+                f"measure{a}{g}",
+                needs + [n for s in range(first, last) for n in arrived(s)],
+                lambda a=a, g=g: measure(a, g),
+                cost=0.1 + 0.15 * (last - first),
+                rank=1 + rank,
+            )
+
+    def total_of(pieces):
+        highest = functools.reduce(jnp.maximum, pieces)
+        return highest + jnp.log(sum(jnp.exp(piece - highest) for piece in pieces))
+
+    def first_part():
+        pieces = range(0, 3 * RING, RING)
+        stats[0:RING] = total_of([sums[k : k + RING] for k in pieces])
+        stats[RING:] = sum(hits[k : k + RING] for k in pieces)
 
     def half_way():
-        highest, total, positive = combined(stats, stats_x)
-        mid[0:RING] = highest
-        mid[RING : 2 * RING] = total
-        mid[2 * RING : 3 * RING] = positive
+        pieces = [stats[...]] + [stats_x[k] for k in range(3)]
+        mid[0:RING] = total_of([piece[:RING] for piece in pieces])
+        mid[RING:] = sum(piece[RING:] for piece in pieces)
 
     def normalise():
-        highest, total, positive = combined(mid, stats_y)
-        log_norm = highest + jnp.log(total)
-        losses = log_norm - positive
+        pieces = [mid[...]] + [stats_y[k] for k in range(3)]
+        log_norm = total_of([piece[:RING] for piece in pieces])
+        for k in range(0, 3 * RING, RING):
+            factor[k : k + RING] = jnp.exp(tops[k : k + RING] - log_norm)
+        losses = log_norm - sum(piece[RING:] for piece in pieces)
         line = lax.broadcasted_iota(jnp.int32, losses.shape, 0)
         losses = jnp.sum(jnp.where(line == place.x, losses, 0.0), axis=0, keepdims=True)
         picked = losses[:, :rows]
         for ys in range(1, RING):
             picked = jnp.where(place.y == ys, losses[:, ys * rows : (ys + 1) * rows], picked)
         loss_out[...] = picked
-        factor[0:RING] = jnp.exp(stats[0:RING] - log_norm)
-
-    def blank():
-        stats[3 * RING :] = jnp.zeros((RING, group), jnp.float32)
-        mid[3 * RING :] = jnp.zeros((RING, group), jnp.float32)
-        factor[RING:] = jnp.zeros((RING, group), jnp.float32)
-
-    plan.task("blank", run=blank)
-    sx = [(f"st_x{k}", "x", k, 16, 0, lambda k=k: (stats, stats_x.at[k - 1])) for k in (1, 2, 3)]
-    sy = [(f"st_y{k}", "y", k, 16, 0, lambda k=k: (mid, stats_y.at[k - 1])) for k in (1, 2, 3)]
+
+    sx = [(f"st_x{k}", "x", k, 8, 0, lambda k=k: (stats, stats_x.at[k - 1])) for k in (1, 2, 3)]
+    sy = [(f"st_y{k}", "y", k, 8, 0, lambda k=k: (mid, stats_y.at[k - 1])) for k in (1, 2, 3)]
     everything = [t[0] for t in plan.tasks]
-    plan.task("sx", everything, sends=sx)
+    plan.task("sx", everything, first_part, sends=sx)
     plan.task("half", [s[0] for s in sx], half_way, sy)
     plan.task("norm", [s[0] for s in sy], normalise)
 
-    def weigh(a):
-        target = target_of(a)
-        scale = factor[pl.ds(at_x(a), 1)]
+    def weigh(a, g):
+        target = targets[pl.ds(at_x(a), 1)]
+        scale = factor[pl.ds(g * RING + at_x(a), 1)]
         lanes = pl.ds(pl.multiple_of(at_x(a) * group, group), group)
 
         def step(b, carry):
@@ -558,7 +608,7 @@
             ).astype(jnp.bfloat16)
             return carry
 
-        lax.fori_loop(0, bands, step, 0)
+        unrolled(*(k * 2 * rows // band for k in groups[g]), step, 0)
 
     def passage_terms(first, last):
         some = weights[first * 2 * rows : last * 2 * rows]
@@ -575,29 +625,46 @@
             (((0,), (0,)), ((), ())),
             preferred_element_type=jnp.float32,
         )
-        qga[at_x(a)] = part[:, : width // 2].reshape(RING, rows, width // 2)
-        qgb[at_x(a)] = part[:, width // 2 :].reshape(RING, rows, width // 2)
-
-    def all_weights():
+        for array, short, lanes in (
+            (qga, qsa, slice(0, width // 2)),
+            (qgb, qsb, slice(width // 2, width)),
+        ):
+            some = part[:, lanes].reshape(RING, rows, width // 2)
+            array[at_x(a)] = some
+            short[at_x(a)] = some.astype(jnp.bfloat16)
+
+    def weights_of(g):
         for a in (2, 1, -1, 0):
-            weigh(a)
-
-    cut = z_size - 3
-    plan.task("weights", ["norm"], all_weights, cost=0.5)
-    plan.task("pterms0", ["weights"], lambda: passage_terms(cut, z_size), cost=0.8)
-    plan.task("qterms2", ["pterms0"], lambda: query_terms(2), cost=0.8, rank=1)
-    plan.task("qterms1", ["qterms2"], lambda: query_terms(1), cost=0.8, rank=2)
+            weigh(a, g)
+
+    cut = z_size - 1
+    plan.task("weights2", ["norm"], lambda: weights_of(2), cost=0.1)
+    plan.task("pterms0", ["weights2"], lambda: passage_terms(cut, z_size), cost=0.4)
+    plan.task("weights1", ["pterms0"], lambda: weights_of(1), cost=0.2)
+    plan.task("weights0", ["weights1"], lambda: weights_of(0), cost=0.3)
+    plan.task("qterms2", ["weights0"], lambda: query_terms(2), cost=0.8, rank=1)
+    plan.task("pterms1", ["qterms2"], lambda: passage_terms(z_size - 3, cut), cost=0.5, rank=1)
+    plan.task("qterms1", ["pterms1"], lambda: query_terms(1), cost=0.8, rank=2)
     plan.task("qterms-1", ["qterms1"], lambda: query_terms(-1), cost=0.8, rank=2)
-    plan.task("pterms1", ["qterms-1"], lambda: passage_terms(0, cut), cost=1.2, rank=3)
-    plan.task("qterms0", ["pterms1"], lambda: query_terms(0), cost=0.8, rank=4)
+    plan.task("pterms2", ["qterms-1"], lambda: passage_terms(0, z_size - 3), cost=1.2, rank=3)
+    plan.task("qterms0", ["pterms2"], lambda: query_terms(0), cost=0.8, rank=4)
 
     def chunk(a):
         return f"qterms{(a + 1) % 4 - 1}"
 
-    end_a = plan_plane_scatter(plan, qga, land_a, late_a, "x", "y", lambda a, b: chunk(a))
-    end_b = plan_plane_scatter(plan, qgb, land_b, late_b, "y", "x", lambda a, b: chunk(b))
+    landing = (far_a, near_a, sum_a)
+    end_a = plan_plane_scatter(plan, qga, qsa, landing, late_a, "x", "y", lambda a, b: chunk(a))
+    landing = (far_b, near_b, sum_b)
+    end_b = plan_plane_scatter(plan, qgb, qsb, landing, late_b, "y", "x", lambda a, b: chunk(b))
     end_p = plan_line_scatter(
-        plan, pg, across, land_z, rows, lambda s: "pterms0" if s >= cut else "pterms1"
+        plan,
+        pg,
+        across,
+        short_z,
+        short_land_z,
+        land_z,
+        rows,
+        lambda s: "pterms0" if s >= cut else ("pterms1" if s >= z_size - 3 else "pterms2"),
     )
 
     def out_a():
@@ -607,7 +674,7 @@
         qg_out[:, width // 2 :] = qgb[place.x, place.y] + late_b[1] + late_b[2]
 
     def out_p():
-        last = z_size // 2 - 1
+        last = z_size // 2 - 2
         pg_out[...] = pg[0, 0] + (land_z[0, last] + land_z[1, last])
 
     plan.task("out_a", end_a, out_a)
@@ -636,7 +703,7 @@
         jax.ShapeDtypeStruct((rows, width), f32),
         jax.ShapeDtypeStruct((rows, width), f32),
     )
-    landing = pltpu.VMEM((3, RING, rows, width // 2), f32)
+    landing = [pltpu.VMEM((RING, rows, width // 2), t) for t in (bf16, bf16, f32)]
     results = pl.pallas_call(
         functools.partial(kernel, zl_size, z_size),
         out_shape=shapes,
@@ -648,20 +715,28 @@
             pltpu.VMEM((RING * RING, 8, 128), jnp.int32),
             pltpu.VMEM((RING * columns, group), f32),
             pltpu.VMEM((columns, RING * group), bf16),
+            pltpu.VMEM((2 * RING, group), jnp.int32),
             pltpu.VMEM((4 * RING, group), f32),
-            pltpu.VMEM((3, 4 * RING, group), f32),
             pltpu.VMEM((4 * RING, group), f32),
-            pltpu.VMEM((3, 4 * RING, group), f32),
+            pltpu.VMEM((4 * RING, group), f32),
             pltpu.VMEM((2 * RING, group), f32),
+            pltpu.VMEM((3, 2 * RING, group), f32),
+            pltpu.VMEM((2 * RING, group), f32),
+            pltpu.VMEM((3, 2 * RING, group), f32),
+            pltpu.VMEM((4 * RING, group), f32),
             pltpu.VMEM((RING, RING, rows, width // 2), f32),
             pltpu.VMEM((RING, RING, rows, width // 2), f32),
+            pltpu.VMEM((RING, RING, rows, width // 2), bf16),
+            pltpu.VMEM((RING, RING, rows, width // 2), bf16),
             pltpu.VMEM((z_size, 2, rows, width), f32),
-            landing,
-            landing,
+            *landing,
+            *landing,
             pltpu.VMEM((3, rows, width // 2), f32),
             pltpu.VMEM((3, rows, width // 2), f32),
             pltpu.VMEM((z_size, rows, width), f32),
-            pltpu.VMEM((2, reach, rows, width), f32),
+            pltpu.VMEM((3, rows, width), bf16),
+            pltpu.VMEM((2, rows, width), bf16),
+            pltpu.VMEM((2, reach - 1, rows, width), f32),
             pltpu.SemaphoreType.DMA((4,)),
             pltpu.SemaphoreType.DMA((SIGNALS,)),
         ],

time: 70.5 us -> 65.9 us (0.935)
  Pallas kernels: 69.7 us -> 65.2 us
    pallas_call x1, Pallas kernels: 67.9 us -> 63.3 us  [body(): pl.pallas_call(functools.partial(kernel, zl_size, z_size), out_shape=shap...]
where the time goes in v3:
time: 65.9 us; the launch traced here: 65.8 us
  Pallas kernels  65.2 us (99%)
    pallas_call x1, Pallas kernels, body(): pl.pallas_call(functools.partial(kernel, zl_size, z_size), out_shape=shap...  63.3 us
    pallas_call x1, Pallas kernels, body(): pl.pallas_call(put_out, out_shape=shapes, in_specs=[pl.BlockSpec(memory_s...  1.85 us

profile of v3, /device:TPU:1, one launch (start us, length us, event | category | flops | bytes accessed | tf_op | source)
XLA Modules:
  0.0 65.8 jit_solution(8466908154289691528)
XLA Ops:
  0.6 63.3 %shard_map.58 = (f32[1,64]{1,0:T(1,128)}, f32[64,1024]{1,0:T(8,128)}, f32[64,1024]{1,0:T(8,128)}) custom-call(f32[64,1024]{1,0:T(8,128)} %q_in.1, f32[64,1024]{1,0:T(8,128)} %p_in.1, s32[1,64]{1,0:T(1,128)} %bitcast.2), custom_call_target="tpu_custom_call" | custom-call | tf_op jit(solution)/shard_map/pallas_call | solution.py:707
  64.0 1.8 %shard_map.59 = (f32[1,64]{1,0:T(1,128)}, f32[64,1024]{1,0:T(8,128)}, f32[64,1024]{1,0:T(8,128)}) custom-call(f32[1,64]{1,0:T(1,128)} %get-tuple-element.9.refs_0_, f32[64,1024]{1,0:T(8,128)} %get-tuple-element.10.refs_1_, f32[64,1024]{1,0:T(8,128)} %get-tuple-element.11.refs_2_), custom_call_target="tpu_custom_call" | custom-call | tf_op jit(solution)/shard_map/pallas_call | solution.py:747

commit v4 on v3

--- a/solution.py
+++ b/solution.py
@@ -14,7 +14,7 @@
 SIGNALS = 144
 
 WIRE = {"x": 0.022, "y": 0.022, "z": 0.022, "c": 0.0016}
-DELAY = {"x": 2.6, "y": 2.6, "z": 2.6, "c": 0.9}
+DELAY = {"x": 2.6, "y": 2.6, "z": 1.5, "c": 0.9}
 
 
 class Place:
@@ -166,10 +166,10 @@
             result.append(s)
         return result
 
-    widest = [s for p in pieces for s in wide(0, p)]
     for p in pieces:
         names["far", p], s = send("g", 0, 0, p, first, 2)
-        widest.append(s)
+        start.append(s)
+    widest = [s for p in pieces for s in wide(0, p)]
     for p in pieces:
         plan.task(f"{first}f-1{p}", [names["f", p, 1]], sends=wide(-1, p))
         plan.task(f"{first}f1{p}", [names["f", p, -1]], sends=wide(1, p))
@@ -384,6 +384,9 @@
     loss_out,
     qg_out,
     pg_out,
+    q_own,
+    p_own,
+    t_own,
     qb,
     pb,
     tb,
@@ -415,6 +418,7 @@
     short_z,
     short_land_z,
     land_z,
+    read_sem,
     send_sem,
     recv_sem,
 ):
@@ -433,9 +437,18 @@
             device_id=place.device(axis, k),
             device_id_type=pl.DeviceIdType.MESH,
         )
-    qb[place.x, place.y] = q_in[...].astype(jnp.bfloat16)
-    pb[0, 0] = p_in[...].astype(jnp.bfloat16)
-    mine = t_in[...]
+    reads = [
+        pltpu.make_async_copy(source, target, read_sem.at[k])
+        for k, (source, target) in enumerate(((p_in, p_own), (q_in, q_own), (t_in, t_own)))
+    ]
+    for read in reads:
+        read.start()
+    reads[0].wait()
+    pb[0, 0] = p_own[...].astype(jnp.bfloat16)
+    reads[1].wait()
+    qb[place.x, place.y] = q_own[...].astype(jnp.bfloat16)
+    reads[2].wait()
+    mine = t_own[...]
     tb[place.x * RING + place.y] = jnp.broadcast_to(
         jnp.concatenate([mine] * (128 // rows), axis=1), (8, 128)
     )
@@ -455,8 +468,8 @@
 
     ty = [(f"tg_y{k}", "y", k, 4, 3, tile) for k in (1, 2, 3)]
     tx = [(f"tg_x{k}", "x", k, 16, 3, tiles) for k in (1, 2, 3)]
-    plan.task("open", sends=start_p + start_a + start_b + ty + wide_a + wide_b, rank=-1)
-    plan.task("ty", [s[0] for s in ty], sends=tx)
+    plan.task("open", sends=ty + start_p + start_a + start_b + wide_a + wide_b, rank=-1)
+    plan.task("ty", [s[0] for s in ty], sends=tx, rank=-1)
 
     def at_x(a):
         return place.at("x", a)
@@ -706,10 +719,13 @@
     landing = [pltpu.VMEM((RING, rows, width // 2), t) for t in (bf16, bf16, f32)]
     results = pl.pallas_call(
         functools.partial(kernel, zl_size, z_size),
-        out_shape=shapes,
-        in_specs=[pl.BlockSpec(memory_space=pltpu.VMEM)] * 3,
+        out_shape=tuple(pltpu.VMEM(s.shape, s.dtype) for s in shapes),
+        in_specs=[pl.BlockSpec(memory_space=pl.ANY)] * 3,
         out_specs=[pl.BlockSpec(memory_space=pltpu.VMEM)] * 3,
         scratch_shapes=[
+            pltpu.VMEM((rows, width), f32),
+            pltpu.VMEM((rows, width), f32),
+            pltpu.VMEM((1, rows), jnp.int32),
             pltpu.VMEM((RING, RING, rows, width), bf16),
             pltpu.VMEM((z_size, 2, rows, width), bf16),
             pltpu.VMEM((RING * RING, 8, 128), jnp.int32),
@@ -737,6 +753,7 @@
             pltpu.VMEM((3, rows, width), bf16),
             pltpu.VMEM((2, rows, width), bf16),
             pltpu.VMEM((2, reach - 1, rows, width), f32),
+            pltpu.SemaphoreType.DMA((3,)),
             pltpu.SemaphoreType.DMA((4,)),
             pltpu.SemaphoreType.DMA((SIGNALS,)),
         ],
@@ -749,7 +766,7 @@
         out_shape=shapes,
         in_specs=[pl.BlockSpec(memory_space=pltpu.VMEM)] * 3,
         out_specs=[pl.BlockSpec(memory_space=pltpu.VMEM)] * 3,
-    )(*results)
+    )(*(pltpu.with_memory_space_constraint(r, pltpu.VMEM) for r in results))
     return losses.reshape(rows), query_grads, passage_grads
 
 

time: 65.9 us -> 63.2 us (0.959)
  Pallas kernels: 65.2 us -> 62.4 us
    pallas_call x1, Pallas kernels: 63.3 us -> 61.6 us  [body(): pl.pallas_call(functools.partial(kernel, zl_size, z_size), out_shape=tupl...]
    pallas_call x1, Pallas kernels: 1.85 us -> 0.83 us  [body(): pl.pallas_call(put_out, out_shape=shapes, in_specs=[pl.BlockSpec(memory_s...]
where the time goes in v4:
time: 63.2 us; the launch traced here: 63.1 us
  Pallas kernels  62.4 us (99%)
  between operations  0.64 us (1%)
    pallas_call x1, Pallas kernels, body(): pl.pallas_call(functools.partial(kernel, zl_size, z_size), out_shape=tupl...  61.6 us

profile of v4, /device:TPU:1, one launch (start us, length us, event | category | flops | bytes accessed | tf_op | source)
XLA Modules:
  0.0 63.1 jit_solution(2851448989013778769)
XLA Ops:
  0.6 61.6 %shard_map.58 = (f32[1,64]{1,0:T(1,128)S(1)}, f32[64,1024]{1,0:T(8,128)S(1)}, f32[64,1024]{1,0:T(8,128)S(1)}) custom-call(f32[64,1024]{1,0:T(8,128)} %q_in.1, f32[64,1024]{1,0:T(8,128)} %p_in.1, s32[1,64]{1,0:T(1,128)} %bitcast.2), custom_call_target="tpu_custom_call" | custom-call | tf_op jit(solution)/shard_map/pallas_call | solution.py:720
  62.3 0.8 %shard_map.59 = (f32[1,64]{1,0:T(1,128)}, f32[64,1024]{1,0:T(8,128)}, f32[64,1024]{1,0:T(8,128)}) custom-call(f32[1,64]{1,0:T(1,128)S(1)} %get-tuple-element.9.refs_0_, f32[64,1024]{1,0:T(8,128)S(1)} %get-tuple-element.10.refs_1_, f32[64,1024]{1,0:T(8,128)S(1)} %get-tuple-element.11.refs_2_), custom_call_target="tpu_custom_call" | custom-call | tf_op jit(solution)/shard_map/pallas_call | solution.py:764

commit v5 on v4

--- a/solution.py
+++ b/solution.py
@@ -11,7 +11,7 @@
 AXES = ("x", "zl", "y", "c", "zh")
 RING = 4
 logit_scale = 20.0
-SIGNALS = 144
+SIGNALS = 160
 
 WIRE = {"x": 0.022, "y": 0.022, "z": 0.022, "c": 0.0016}
 DELAY = {"x": 2.6, "y": 2.6, "z": 1.5, "c": 0.9}
@@ -28,6 +28,8 @@
         return lax.rem(getattr(self, axis) + (offset % size), size)
 
     def device(self, axis, offset):
+        if axis == "xy":
+            return {"x": self.at("x", offset[0]), "y": self.at("y", offset[1])}
         place = self.at(axis, offset)
         if axis == "z":
             return {"zl": lax.rem(place, self.zl_size), "zh": lax.div(place, self.zl_size)}
@@ -64,6 +66,9 @@
                         link[lane] = max(link.get(lane, 0.0), now) + kib * WIRE[axis]
                     known[message] = max(link[axis, 1], link[axis, -1]) + DELAY[axis] + 0.6
                     continue
+                if axis == "xy":
+                    known[message] = now + 4.5
+                    continue
                 far = abs(offset)
                 lane = (axis, offset // far)
                 link[lane] = max(link.get(lane, 0.0), now) + kib * WIRE[axis] * far
@@ -78,7 +83,7 @@
             kind = "qg"
         group = self.slots.setdefault(message.split("_")[0], {})
         number = group.setdefault(message, len(group))
-        base = {"qg": 0, "pg": 60, "tg": 96, "st": 102, "rz": 108}[kind]
+        base = {"qg": 0, "pg": 60, "tg": 96, "ht": 102, "rz": 108, "st": 144}[kind]
         return self.recv_sem.at[base + number]
 
     def run(self):
@@ -397,10 +402,13 @@
     sums,
     hits,
     stats,
-    stats_x,
-    mid,
-    stats_y,
+    stats_all,
+    hit_own,
+    hit_x,
+    hit_mid,
+    hit_y,
     factor,
+    norms,
     qga,
     qgb,
     qsa,
@@ -428,6 +436,7 @@
     columns = 2 * z_size * rows
     place = Place(zl_size, z_size)
     peers = [("x", k) for k in (1, 2, 3)] + [("y", k) for k in (1, 2, 3)]
+    peers += [("xy", (a, b)) for a in (1, 2, 3) for b in (1, 2, 3)]
     peers += [("z", k) for k in (1, 2, z_size - 2, z_size - 1)] + [("c", 1)]
     barrier = pltpu.get_barrier_semaphore()
     for axis, k in peers:
@@ -474,7 +483,7 @@
     def at_x(a):
         return place.at("x", a)
 
-    groups = ((0, z_size // 2), (z_size // 2, z_size - 1), (z_size - 1, z_size))
+    groups = ((0, z_size // 2), (z_size // 2, z_size))
 
     def multiply(a, g):
         first, last = groups[g]
@@ -578,22 +587,29 @@
         highest = functools.reduce(jnp.maximum, pieces)
         return highest + jnp.log(sum(jnp.exp(piece - highest) for piece in pieces))
 
+    def pack(ref, value):
+        ref[0:RING] = value[:, : group // 2]
+        ref[RING:] = value[:, group // 2 :]
+
+    def unpack(value):
+        return jnp.concatenate([value[:RING], value[RING:]], axis=1)
+
     def first_part():
-        pieces = range(0, 3 * RING, RING)
-        stats[0:RING] = total_of([sums[k : k + RING] for k in pieces])
-        stats[RING:] = sum(hits[k : k + RING] for k in pieces)
+        pieces = range(0, len(groups) * RING, RING)
+        pack(stats, total_of([sums[k : k + RING] for k in pieces]))
+        pack(hit_own, sum(hits[k : k + RING] for k in pieces))
+
+    def normalise():
+        norms[...] = total_of([stats[...]] + [stats_all[k] for k in range(RING * RING - 1)])
+        log_norm = unpack(norms[...])
+        for k in range(0, len(groups) * RING, RING):
+            factor[k : k + RING] = jnp.exp(tops[k : k + RING] - log_norm)
 
     def half_way():
-        pieces = [stats[...]] + [stats_x[k] for k in range(3)]
-        mid[0:RING] = total_of([piece[:RING] for piece in pieces])
-        mid[RING:] = sum(piece[RING:] for piece in pieces)
-
-    def normalise():
-        pieces = [mid[...]] + [stats_y[k] for k in range(3)]
-        log_norm = total_of([piece[:RING] for piece in pieces])
-        for k in range(0, 3 * RING, RING):
-            factor[k : k + RING] = jnp.exp(tops[k : k + RING] - log_norm)
-        losses = log_norm - sum(piece[RING:] for piece in pieces)
+        hit_mid[...] = hit_own[...] + sum(hit_x[k] for k in range(3))
+
+    def put_losses():
+        losses = unpack(norms[...] - hit_mid[...] - sum(hit_y[k] for k in range(3)))
         line = lax.broadcasted_iota(jnp.int32, losses.shape, 0)
         losses = jnp.sum(jnp.where(line == place.x, losses, 0.0), axis=0, keepdims=True)
         picked = losses[:, :rows]
@@ -601,14 +617,23 @@
             picked = jnp.where(place.y == ys, losses[:, ys * rows : (ys + 1) * rows], picked)
         loss_out[...] = picked
 
-    sx = [(f"st_x{k}", "x", k, 8, 0, lambda k=k: (stats, stats_x.at[k - 1])) for k in (1, 2, 3)]
-    sy = [(f"st_y{k}", "y", k, 8, 0, lambda k=k: (mid, stats_y.at[k - 1])) for k in (1, 2, 3)]
+    others = [(a, b) for a in range(RING) for b in range(RING) if a or b]
+    others.sort(key=lambda o: -min(o[0], RING - o[0]) - min(o[1], RING - o[1]))
+    spread = []
+    for number, (a, b) in enumerate(others):
+        axis, offset = ("xy", (a, b)) if a and b else (("x", a) if a else ("y", b))
+        refs = lambda number=number: (stats, stats_all.at[number])
+        spread.append((f"st_{a}{b}", axis, offset, 4, 4, refs))
+    hx = [(f"ht_x{k}", "x", k, 4, 0, lambda k=k: (hit_own, hit_x.at[k - 1])) for k in (1, 2, 3)]
+    hy = [(f"ht_y{k}", "y", k, 4, 0, lambda k=k: (hit_mid, hit_y.at[k - 1])) for k in (1, 2, 3)]
     everything = [t[0] for t in plan.tasks]
-    plan.task("sx", everything, first_part, sends=sx)
-    plan.task("half", [s[0] for s in sx], half_way, sy)
-    plan.task("norm", [s[0] for s in sy], normalise)
-
-    def weigh(a, g):
+    plan.task("spread", everything, first_part, sends=spread + hx)
+    plan.task("norm", [m[0] for m in spread], normalise, rank=-1)
+    plan.task("half", ["norm"] + [m[0] for m in hx], half_way, hy, rank=8)
+    plan.task("losses", [m[0] for m in hy], put_losses, rank=9)
+
+    def weigh(a, first, last):
+        g = 0 if last <= z_size // 2 else 1
         target = targets[pl.ds(at_x(a), 1)]
         scale = factor[pl.ds(g * RING + at_x(a), 1)]
         lanes = pl.ds(pl.multiple_of(at_x(a) * group, group), group)
@@ -621,7 +646,7 @@
             ).astype(jnp.bfloat16)
             return carry
 
-        unrolled(*(k * 2 * rows // band for k in groups[g]), step, 0)
+        unrolled(first * 2 * rows // band, last * 2 * rows // band, step, 0)
 
     def passage_terms(first, last):
         some = weights[first * 2 * rows : last * 2 * rows]
@@ -646,15 +671,15 @@
             array[at_x(a)] = some
             short[at_x(a)] = some.astype(jnp.bfloat16)
 
-    def weights_of(g):
+    def weights_of(first, last):
         for a in (2, 1, -1, 0):
-            weigh(a, g)
+            weigh(a, first, last)
 
     cut = z_size - 1
-    plan.task("weights2", ["norm"], lambda: weights_of(2), cost=0.1)
+    plan.task("weights2", ["norm"], lambda: weights_of(cut, z_size), cost=0.1)
     plan.task("pterms0", ["weights2"], lambda: passage_terms(cut, z_size), cost=0.4)
-    plan.task("weights1", ["pterms0"], lambda: weights_of(1), cost=0.2)
-    plan.task("weights0", ["weights1"], lambda: weights_of(0), cost=0.3)
+    plan.task("weights1", ["pterms0"], lambda: weights_of(z_size // 2, cut), cost=0.2)
+    plan.task("weights0", ["weights1"], lambda: weights_of(0, z_size // 2), cost=0.3)
     plan.task("qterms2", ["weights0"], lambda: query_terms(2), cost=0.8, rank=1)
     plan.task("pterms1", ["qterms2"], lambda: passage_terms(z_size - 3, cut), cost=0.5, rank=1)
     plan.task("qterms1", ["pterms1"], lambda: query_terms(1), cost=0.8, rank=2)
@@ -698,6 +723,7 @@
     plan.finish(scores, 1)
     plan.finish(scores, 2)
     plan.finish(tb, 3, per_kib=4)
+    plan.finish(tb, 4, per_kib=4)
 
 
 def put_out(*refs):
@@ -716,6 +742,7 @@
         jax.ShapeDtypeStruct((rows, width), f32),
         jax.ShapeDtypeStruct((rows, width), f32),
     )
+    line = pltpu.VMEM((2 * RING, group // 2), f32)
     landing = [pltpu.VMEM((RING, rows, width // 2), t) for t in (bf16, bf16, f32)]
     results = pl.pallas_call(
         functools.partial(kernel, zl_size, z_size),
@@ -735,11 +762,14 @@
             pltpu.VMEM((4 * RING, group), f32),
             pltpu.VMEM((4 * RING, group), f32),
             pltpu.VMEM((4 * RING, group), f32),
-            pltpu.VMEM((2 * RING, group), f32),
-            pltpu.VMEM((3, 2 * RING, group), f32),
-            pltpu.VMEM((2 * RING, group), f32),
-            pltpu.VMEM((3, 2 * RING, group), f32),
+            line,
+            pltpu.VMEM((RING * RING - 1, 2 * RING, group // 2), f32),
+            line,
+            pltpu.VMEM((3, 2 * RING, group // 2), f32),
+            line,
+            pltpu.VMEM((3, 2 * RING, group // 2), f32),
             pltpu.VMEM((4 * RING, group), f32),
+            line,
             pltpu.VMEM((RING, RING, rows, width // 2), f32),
             pltpu.VMEM((RING, RING, rows, width // 2), f32),
             pltpu.VMEM((RING, RING, rows, width // 2), bf16),
@@ -754,7 +784,7 @@
             pltpu.VMEM((2, rows, width), bf16),
             pltpu.VMEM((2, reach - 1, rows, width), f32),
             pltpu.SemaphoreType.DMA((3,)),
-            pltpu.SemaphoreType.DMA((4,)),
+            pltpu.SemaphoreType.DMA((5,)),
             pltpu.SemaphoreType.DMA((SIGNALS,)),
         ],
         compiler_params=pltpu.CompilerParams(

time: 63.2 us -> 61.7 us (0.976)
  Pallas kernels: 62.4 us -> 61 us
    pallas_call x1, Pallas kernels: 61.6 us -> 60.1 us  [body(): pl.pallas_call(functools.partial(kernel, zl_size, z_size), out_shape=tupl...]
where the time goes in v5:
time: 61.7 us; the launch traced here: 61.6 us
  Pallas kernels  61 us (99%)
  between operations  0.64 us (1%)
    pallas_call x1, Pallas kernels, body(): pl.pallas_call(functools.partial(kernel, zl_size, z_size), out_shape=tupl...  60.1 us

profile of v5, /device:TPU:1, one launch (start us, length us, event | category | flops | bytes accessed | tf_op | source)
XLA Modules:
  0.0 61.6 jit_solution(8953329576909415281)
XLA Ops:
  0.6 60.1 %shard_map.58 = (f32[1,64]{1,0:T(1,128)S(1)}, f32[64,1024]{1,0:T(8,128)S(1)}, f32[64,1024]{1,0:T(8,128)S(1)}) custom-call(f32[64,1024]{1,0:T(8,128)} %q_in.1, f32[64,1024]{1,0:T(8,128)} %p_in.1, s32[1,64]{1,0:T(1,128)} %bitcast.2), custom_call_target="tpu_custom_call" | custom-call | tf_op jit(solution)/shard_map/pallas_call | solution.py:747
  60.8 0.8 %shard_map.59 = (f32[1,64]{1,0:T(1,128)}, f32[64,1024]{1,0:T(8,128)}, f32[64,1024]{1,0:T(8,128)}) custom-call(f32[1,64]{1,0:T(1,128)S(1)} %get-tuple-element.9.refs_0_, f32[64,1024]{1,0:T(8,128)S(1)} %get-tuple-element.10.refs_1_, f32[64,1024]{1,0:T(8,128)S(1)} %get-tuple-element.11.refs_2_), custom_call_target="tpu_custom_call" | custom-call | tf_op jit(solution)/shard_map/pallas_call | solution.py:794

commit v6 on v5

--- a/solution.py
+++ b/solution.py
@@ -679,10 +679,10 @@
     plan.task("weights2", ["norm"], lambda: weights_of(cut, z_size), cost=0.1)
     plan.task("pterms0", ["weights2"], lambda: passage_terms(cut, z_size), cost=0.4)
     plan.task("weights1", ["pterms0"], lambda: weights_of(z_size // 2, cut), cost=0.2)
-    plan.task("weights0", ["weights1"], lambda: weights_of(0, z_size // 2), cost=0.3)
+    plan.task("weights0", ["pterms1"], lambda: weights_of(0, z_size // 2), cost=0.3)
     plan.task("qterms2", ["weights0"], lambda: query_terms(2), cost=0.8, rank=1)
-    plan.task("pterms1", ["qterms2"], lambda: passage_terms(z_size - 3, cut), cost=0.5, rank=1)
-    plan.task("qterms1", ["pterms1"], lambda: query_terms(1), cost=0.8, rank=2)
+    plan.task("pterms1", ["weights1"], lambda: passage_terms(z_size - 3, cut), cost=0.5, rank=1)
+    plan.task("qterms1", ["qterms2"], lambda: query_terms(1), cost=0.8, rank=2)
     plan.task("qterms-1", ["qterms1"], lambda: query_terms(-1), cost=0.8, rank=2)
     plan.task("pterms2", ["qterms-1"], lambda: passage_terms(0, z_size - 3), cost=1.2, rank=3)
     plan.task("qterms0", ["pterms2"], lambda: query_terms(0), cost=0.8, rank=4)

time: 61.7 us -> 61.3 us (level)
  no operation moved by 1% of the time
where the time goes in v6:
time: 61.3 us; the launch traced here: 61.2 us
  Pallas kernels  60.5 us (99%)
  between operations  0.64 us (1%)
    pallas_call x1, Pallas kernels, body(): pl.pallas_call(functools.partial(kernel, zl_size, z_size), out_shape=tupl...  59.7 us

profile of v6, /device:TPU:1, one launch (start us, length us, event | category | flops | bytes accessed | tf_op | source)
XLA Modules:
  0.0 61.2 jit_solution(4753261279160752634)
XLA Ops:
  0.6 59.7 %shard_map.58 = (f32[1,64]{1,0:T(1,128)S(1)}, f32[64,1024]{1,0:T(8,128)S(1)}, f32[64,1024]{1,0:T(8,128)S(1)}) custom-call(f32[64,1024]{1,0:T(8,128)} %q_in.1, f32[64,1024]{1,0:T(8,128)} %p_in.1, s32[1,64]{1,0:T(1,128)} %bitcast.2), custom_call_target="tpu_custom_call" | custom-call | tf_op jit(solution)/shard_map/pallas_call | solution.py:747
  60.4 0.8 %shard_map.59 = (f32[1,64]{1,0:T(1,128)}, f32[64,1024]{1,0:T(8,128)}, f32[64,1024]{1,0:T(8,128)}) custom-call(f32[1,64]{1,0:T(1,128)S(1)} %get-tuple-element.9.refs_0_, f32[64,1024]{1,0:T(8,128)S(1)} %get-tuple-element.10.refs_1_, f32[64,1024]{1,0:T(8,128)S(1)} %get-tuple-element.11.refs_2_), custom_call_target="tpu_custom_call" | custom-call | tf_op jit(solution)/shard_map/pallas_call | solution.py:794
